TPU v7x, 128 devices: a whole 4x4x4 slice. The times are simulated.
128 devices in a mesh: gz: 16 (over z, x_lo, core), pair: 8 (over x_hi, y).
Axes of the slice: x: 4 (x_hi: 2, x_lo: 2; x = x_hi * 2 + x_lo), y: 4, z: 4, core: 2. Of those that a mesh axis runs over, the one named last changes fastest.
Arguments:
- orbitals: bfloat16 [8, 128, 256, 256], P(None, 'gz'), may hold values from -6 to 6
- pair_index: int32 [8, 2], P('pair'), may hold values from 0 to 7
- pair_weight: float32 [8], P('pair'), may hold values from 0.5 to 2
Outputs:
- potential: float32 [8, 128, 256, 256], P('pair', 'gz')
- residual_norm: float32 [8], P('pair')
- energy: float32 [1], replicated
Inputs may be any that keep to these rules, and one draw needn't show every extreme that they name: `pair_index`: A pair may name one orbital twice.
All inputs are finite; a program needn't handle non-finite values.
Results may differ from a plain program's by a relative error of at most 0.0003.
Values sent between devices are 32-bit elements; how exact they have to be, the bound alone decides.
A program may use at most 320 MiB of HBM per device.

v0:
```python
import jax
import jax.numpy as jnp
from jax import lax
from jax.sharding import PartitionSpec as P

LEVELS = 4
NU = 2
COARSE = 8


relax = 2.0 / 3.0


def with_halo(block, sides, width):
    for axis, dim in sides:
        count = lax.axis_size(axis)
        forward = [(i, i + 1) for i in range(count - 1)]
        backward = [(target, source) for source, target in forward]
        low = lax.ppermute(
            lax.slice_in_dim(block, block.shape[dim] - width, None, axis=dim), axis, forward
        )
        high = lax.ppermute(lax.slice_in_dim(block, 0, width, axis=dim), axis, backward)
        block = jnp.concatenate([low, block, high], axis=dim)
    return block


def laid_out(pieces, dim):
    shape = list(pieces.shape[1:])
    shape[dim] *= pieces.shape[0]
    return jnp.moveaxis(pieces, 0, dim).reshape(shape)


def copy_for_each(array, axis):
    peers = lax.axis_size(axis)
    return lax.all_to_all(
        jnp.broadcast_to(array[None], (peers, *array.shape)), axis, 0, 0, tiled=True
    )


def gather_directly(array, axis, dim):
    return laid_out(copy_for_each(array, axis), dim)


def of_everyone(array, axis):
    return copy_for_each(array, axis).sum(axis=0)


def packed_total(arrays, axis):
    ends = [0]
    for a in arrays:
        ends.append(ends[-1] + a.size)
    total = of_everyone(jnp.concatenate([a.ravel() for a in arrays]), axis)
    return tuple((total[b:e].reshape(a.shape) for a, b, e in zip(arrays, ends, ends[1:])))


def apply_op(field, level):
    extended = with_halo(field, (("gz", 1),), 1)
    padded = jnp.pad(field, ((0, 0), (0, 0), (1, 1), (1, 1)))
    beside = extended[:, 2:] + extended[:, :-2]
    beside = beside + padded[:, :, 2:, 1:-1] + padded[:, :, :-2, 1:-1]
    beside = beside + padded[:, :, 1:-1, 2:] + padded[:, :, 1:-1, :-2]
    return (6.0 * field - beside) * 0.25**level


def local_op(field, level):
    padded = jnp.pad(field, ((0, 0), (1, 1), (1, 1), (1, 1)))
    beside = padded[:, 2:, 1:-1, 1:-1] + padded[:, :-2, 1:-1, 1:-1]
    beside = beside + padded[:, 1:-1, 2:, 1:-1] + padded[:, 1:-1, :-2, 1:-1]
    beside = beside + padded[:, 1:-1, 1:-1, 2:] + padded[:, 1:-1, 1:-1, :-2]
    return (6.0 * field - beside) * 0.25**level


def sweep(field, source, level):
    return field + (source - apply_op(field, level)) * (relax * 4.0**level / 6.0)


def restrict(field):
    pairs, zsize, ysize, xsize = field.shape
    return field.reshape(pairs, zsize // 2, 2, ysize // 2, 2, xsize // 2, 2).mean(axis=(2, 4, 6))


def prolong(field):
    return jnp.repeat(jnp.repeat(jnp.repeat(field, 2, axis=1), 2, axis=2), 2, axis=3)


def coarsest(source, level):
    gathered = gather_directly(source, "gz", 1)
    field = jnp.zeros_like(gathered)
    for _ in range(COARSE):
        field = field + (gathered - local_op(field, level)) * (relax * 4.0**level / 6.0)
    planes = source.shape[1]
    return lax.dynamic_slice_in_dim(field, lax.axis_index("gz") * planes, planes, 1)


def vcycle(field, source, level):
    if level == LEVELS - 1:
        return coarsest(source, level)
    for _ in range(NU):
        field = sweep(field, source, level)
    remain = source - apply_op(field, level)
    coarse_source = restrict(remain)
    correction = vcycle(jnp.zeros_like(coarse_source), coarse_source, level + 1)
    field = field + prolong(correction)
    for _ in range(NU):
        field = sweep(field, source, level)
    return field


def solve(density):
    field = jnp.zeros_like(density)
    field = vcycle(field, density, 0)
    return field


def per_device(orbitals, pair_index, pair_weight):
    left_orbital = jnp.take(orbitals, pair_index[:, 0], axis=0).astype(jnp.float32)
    right_orbital = jnp.take(orbitals, pair_index[:, 1], axis=0).astype(jnp.float32)
    density = left_orbital * right_orbital
    potential = solve(density)
    final = density - apply_op(potential, 0)
    totals = packed_total(
        (jnp.sum(final * final, axis=(1, 2, 3)), jnp.sum(density * potential, axis=(1, 2, 3))), "gz"
    )
    cell_count = density.shape[1] * lax.axis_size("gz") * density.shape[2] * density.shape[3]
    residual_norm = jnp.sqrt(totals[0] / cell_count)
    partial_energy = -0.5 * jnp.sum(pair_weight * totals[1]) / cell_count
    energy = of_everyone(partial_energy, "pair").reshape(1)
    return (potential, residual_norm, energy)


def solution(mesh):
    return jax.shard_map(
        per_device,
        mesh=mesh,
        in_specs=(P(None, "gz", None, None), P("pair", None), P("pair")),
        out_specs=(P("pair", "gz", None, None), P("pair"), P()),
        check_vma=False,
    )
```

profile of v0, /device:TPU:1, one launch (start us, length us, event | category | flops | bytes accessed | tf_op | source)
XLA Modules:
  0.0 420.6 jit_solution(9914910534957309060)
XLA Ops:
  1.5 3.3 collective-permute-start
  22.0 3.6 collective-permute-start.3
  33.5 4.4 %collective-permute-start.5 = (f32[1,1,256,256]{2,1,3,0:T(1,128)S(1)}, f32[1,1,256,256]{2,1,3,0:T(1,128)S(1)}, u32[]{:S(2)}, u32[]{:S(2)}) collective-permute-start(f32[1,1,256,256]{2,1,3,0:T(1,128)S(1)} %get-tuple-element.45), channel_id=1, source_target_pairs={{0,8},{8,16},{16,24},{24,32},{32,40},{40,48},{48,56},{56,64},{64,7... | collective-permute-start | bytes 786440 | tf_op jit(solution)/shard_map/ppermute | solution.py:19
  39.9 3.6 collective-permute-start.7
  49.5 136.2 %reshape.109 = f32[4,2,128,2,128,2]{5,4,3,2,1,0:T(8,128)} reshape(f32[1,8,256,256]{3,2,1,0:T(8,128)} %copy.44) | data formatting | bytes 4194304 | tf_op jit(solution)/shard_map/reshape | solution.py:79
  185.7 40.6 %reduce_sum.78 = f32[4,128,128]{2,1,0:T(8,128)S(1)} reduce(f32[4,2,128,2,128,2]{5,4,3,2,1,0:T(8,128)} %reshape.109, f32[]{:T(128)} %constant.30.clone.1), dimensions={1,3,5}, to_apply=%region_0.0 | reduce | flops 458752 | bytes 2359300 | tf_op jit(solution)/shard_map/reduce_sum | solution.py:79
  228.5 4.4 %collective-permute-start.9 = (f32[1,1,128,128]{3,2,1,0:T(8,128)S(1)}, f32[1,1,128,128]{3,2,1,0:T(8,128)S(1)}, u32[]{:S(2)}, u32[]{:S(2)}) collective-permute-start(f32[1,1,128,128]{3,2,1,0:T(8,128)S(1)} %get-tuple-element.57), channel_id=1, source_target_pairs={{0,8},{8,16},{16,24},{24,32},{32,40},{40,48},{48,56},{56,64},{64,7... | collective-permute-start | bytes 196616 | tf_op jit(solution)/shard_map/ppermute | solution.py:19
  236.5 4.3 %collective-permute-start.11 = (f32[1,1,128,128]{3,2,1,0:T(8,128)S(1)}, f32[1,1,128,128]{3,2,1,0:T(8,128)S(1)}, u32[]{:S(2)}, u32[]{:S(2)}) collective-permute-start(f32[1,1,128,128]{3,2,1,0:T(8,128)S(1)} %get-tuple-element.55), channel_id=1, source_target_pairs={{0,8},{8,16},{16,24},{24,32},{32,40},{40,48},{48,56},{56,64},{64,7... | collective-permute-start | bytes 196616 | tf_op jit(solution)/shard_map/ppermute | solution.py:19
  242.7 4.8 %collective-permute-start.13 = (f32[1,1,64,64]{3,2,1,0:T(8,128)S(1)}, f32[1,1,64,64]{3,2,1,0:T(8,128)S(1)}, u32[]{:S(2)}, u32[]{:S(2)}) collective-permute-start(f32[1,1,64,64]{3,2,1,0:T(8,128)S(1)} %broadcast.210), channel_id=1, source_target_pairs={{0,8},{8,16},{16,24},{24,32},{32,40},{40,48},{48,56},{56,64},{64,7... | collective-permute-start | bytes 49160 | tf_op jit(solution)/shard_map/ppermute | solution.py:19
  247.7 18.1 %reshape.110 = f32[2,2,64,2,64,2]{5,4,3,2,1,0:T(8,128)} reshape(f32[1,4,128,128]{3,2,1,0:T(8,128)S(1)} %fusion.137) | data formatting | bytes 524288 | tf_op jit(solution)/shard_map/reshape | solution.py:79
  265.8 7.0 %reduce_sum.79 = f32[2,64,64]{2,1,0:T(8,128)S(1)} reduce(f32[2,2,64,2,64,2]{5,4,3,2,1,0:T(8,128)} %reshape.110, f32[]{:T(128)} %constant.30.clone.1), dimensions={1,3,5}, to_apply=%region_1.3 | reduce | flops 57344 | bytes 294916 | tf_op jit(solution)/shard_map/reduce_sum | solution.py:79
  274.9 5.2 %collective-permute-start.15 = (f32[1,1,64,64]{3,2,1,0:T(8,128)S(1)}, f32[1,1,64,64]{3,2,1,0:T(8,128)S(1)}, u32[]{:S(2)}, u32[]{:S(2)}) collective-permute-start(f32[1,1,64,64]{3,2,1,0:T(8,128)S(1)} %get-tuple-element.65), channel_id=1, source_target_pairs={{0,8},{8,16},{16,24},{24,32},{32,40},{40,48},{48,56},{56,64},{64,7... | collective-permute-start | bytes 49160 | tf_op jit(solution)/shard_map/ppermute | solution.py:19
  283.2 4.6 %collective-permute-start.17 = (f32[1,1,64,64]{3,2,1,0:T(8,128)S(1)}, f32[1,1,64,64]{3,2,1,0:T(8,128)S(1)}, u32[]{:S(2)}, u32[]{:S(2)}) collective-permute-start(f32[1,1,64,64]{3,2,1,0:T(8,128)S(1)} %get-tuple-element.63), channel_id=1, source_target_pairs={{0,8},{8,16},{16,24},{24,32},{32,40},{40,48},{48,56},{56,64},{64,7... | collective-permute-start | bytes 49160 | tf_op jit(solution)/shard_map/ppermute | solution.py:19
  292.2 11.7 %all-to-all-start = ((f32[16,1,1024]{2,1,0:T(1,128)}), f32[16,1,1024]{2,1,0:T(1,128)S(1)}, u32[]{:S(2)}, u32[]{:S(2)}) async-start(f32[16,1,1024]{2,1,0:T(1,128)} %reshape.153), calls=%async_computation | async-start | bytes 131072 | tf_op jit(solution)/shard_map/all_to_all | solution.py:35
  303.9 5.8 %all-to-all-done = f32[16,1,1024]{2,1,0:T(1,128)S(1)} async-done(((f32[16,1,1024]{2,1,0:T(1,128)}), f32[16,1,1024]{2,1,0:T(1,128)S(1)}, u32[]{:S(2)}, u32[]{:S(2)}) %all-to-all-start) | async-done | bytes 65568 | tf_op jit(solution)/shard_map/all_to_all | solution.py:35
  322.0 4.2 %collective-permute-start.21 = (f32[1,1,64,64]{3,2,1,0:T(8,128)S(1)}, f32[1,1,64,64]{3,2,1,0:T(8,128)S(1)}, u32[]{:S(2)}, u32[]{:S(2)}) collective-permute-start(f32[1,1,64,64]{3,2,1,0:T(8,128)S(1)} %get-tuple-element.59), channel_id=1, source_target_pairs={{0,8},{8,16},{16,24},{24,32},{32,40},{40,48},{48,56},{56,64},{64,7... | collective-permute-start | bytes 49160 | tf_op jit(solution)/shard_map/ppermute | solution.py:19
  329.8 4.2 %collective-permute-start.23 = (f32[1,1,128,128]{3,2,1,0:T(8,128)S(1)}, f32[1,1,128,128]{3,2,1,0:T(8,128)S(1)}, u32[]{:S(2)}, u32[]{:S(2)}) collective-permute-start(f32[1,1,128,128]{3,2,1,0:T(8,128)S(1)} %get-tuple-element.51), channel_id=1, source_target_pairs={{0,8},{8,16},{16,24},{24,32},{32,40},{40,48},{48,56},{56,64},{64,7... | collective-permute-start | bytes 196616 | tf_op jit(solution)/shard_map/ppermute | solution.py:19
  337.5 4.3 %collective-permute-start.25 = (f32[1,1,128,128]{3,2,1,0:T(8,128)S(1)}, f32[1,1,128,128]{3,2,1,0:T(8,128)S(1)}, u32[]{:S(2)}, u32[]{:S(2)}) collective-permute-start(f32[1,1,128,128]{3,2,1,0:T(8,128)S(1)} %get-tuple-element.49), channel_id=1, source_target_pairs={{0,8},{8,16},{16,24},{24,32},{32,40},{40,48},{48,56},{56,64},{64,7... | collective-permute-start | bytes 196616 | tf_op jit(solution)/shard_map/ppermute | solution.py:19
  350.5 4.3 %collective-permute-start.27 = (f32[1,1,256,256]{2,1,3,0:T(1,128)S(1)}, f32[1,1,256,256]{2,1,3,0:T(1,128)S(1)}, u32[]{:S(2)}, u32[]{:S(2)}) collective-permute-start(f32[1,1,256,256]{2,1,3,0:T(1,128)S(1)} %get-tuple-element.43), channel_id=1, source_target_pairs={{0,8},{8,16},{16,24},{24,32},{32,40},{40,48},{48,56},{56,64},{64,7... | collective-permute-start | bytes 786440 | tf_op jit(solution)/shard_map/ppermute | solution.py:19
  362.5 4.4 %collective-permute-start.29 = (f32[1,1,256,256]{2,1,3,0:T(1,128)S(1)}, f32[1,1,256,256]{2,1,3,0:T(1,128)S(1)}, u32[]{:S(2)}, u32[]{:S(2)}) collective-permute-start(f32[1,1,256,256]{2,1,3,0:T(1,128)S(1)} %get-tuple-element.41), channel_id=1, source_target_pairs={{0,8},{8,16},{16,24},{24,32},{32,40},{40,48},{48,56},{56,64},{64,7... | collective-permute-start | bytes 786440 | tf_op jit(solution)/shard_map/ppermute | solution.py:19
  374.7 4.4 %collective-permute-start.31 = (f32[1,1,256,256]{2,1,3,0:T(1,128)S(1)}, f32[1,1,256,256]{2,1,3,0:T(1,128)S(1)}, u32[]{:S(2)}, u32[]{:S(2)}) collective-permute-start(f32[1,1,256,256]{2,1,3,0:T(1,128)S(1)} %get-tuple-element.39), channel_id=1, source_target_pairs={{0,8},{8,16},{16,24},{24,32},{32,40},{40,48},{48,56},{56,64},{64,7... | collective-permute-start | bytes 786440 | tf_op jit(solution)/shard_map/ppermute | solution.py:19
  387.3 11.2 %all-to-all-start.1 = ((f32[16,1,2]{2,1,0:T(1,128)}), f32[16,1,2]{2,1,0:T(1,128)S(1)}, u32[]{:S(2)}, u32[]{:S(2)}) async-start(f32[16,1,2]{2,1,0:T(1,128)} %broadcast_in_dim.88), calls=%async_computation.1 | async-start | bytes 16384 | tf_op jit(solution)/shard_map/all_to_all | solution.py:35
  405.9 6.4 %all-to-all-start.2 = ((f32[8,1,1]{2,1,0:T(1,128)}), f32[8,1,1]{2,1,0:T(1,128)S(1)}, u32[]{:S(2)}, u32[]{:S(2)}) async-start(f32[8,1,1]{2,1,0:T(1,128)} %broadcast_in_dim.89), calls=%async_computation.2 | async-start | bytes 8192 | tf_op jit(solution)/shard_map/all_to_all | solution.py:35
  413.0 5.8 %all-to-all-done.2 = f32[8,1,1]{2,1,0:T(1,128)S(1)} async-done(((f32[8,1,1]{2,1,0:T(1,128)}), f32[8,1,1]{2,1,0:T(1,128)S(1)}, u32[]{:S(2)}, u32[]{:S(2)}) %all-to-all-start.2) | async-done | bytes 64 | tf_op jit(solution)/shard_map/all_to_all | solution.py:35
  (139 shorter events, 105.2 us)
Async XLA Ops:
  1.5 15.4 %collective-permute-start = (f32[1,1,256,256]{2,1,3,0:T(1,128)}, f32[1,1,256,256]{2,1,3,0:T(1,128)S(1)}, u32[]{:S(2)}, u32[]{:S(2)}) collective-permute-start(f32[1,1,256,256]{2,1,3,0:T(1,128)} %broadcast.201), channel_id=1, source_target_pairs={{8,0},{16,8},{24,16},{32,24},{40,32},{48,40},{56,48},{64,56},{72,6... | collective-permute-start | bytes 786440 | tf_op jit(solution)/shard_map/ppermute | solution.py:22
  4.8 12.1 %collective-permute-start.1 = (f32[1,1,256,256]{2,1,3,0:T(1,128)}, f32[1,1,256,256]{2,1,3,0:T(1,128)}, u32[]{:S(2)}, u32[]{:S(2)}) collective-permute-start(f32[1,1,256,256]{2,1,3,0:T(1,128)} %broadcast.201), channel_id=1, source_target_pairs={{0,8},{8,16},{16,24},{24,32},{32,40},{40,48},{48,56},{56,64},{64,7... | collective-permute-start | bytes 786440 | tf_op jit(solution)/shard_map/ppermute | solution.py:19
  20.1 7.7 %collective-permute-start.2 = (f32[1,1,256,256]{2,1,3,0:T(1,128)S(1)}, f32[1,1,256,256]{2,1,3,0:T(1,128)S(1)}, u32[]{:S(2)}, u32[]{:S(2)}) collective-permute-start(f32[1,1,256,256]{2,1,3,0:T(1,128)S(1)} %get-tuple-element.46), channel_id=1, source_target_pairs={{8,0},{16,8},{24,16},{32,24},{40,32},{48,40},{56,48},{64,56},{72,6... | collective-permute-start | bytes 786440 | tf_op jit(solution)/shard_map/ppermute | solution.py:22
  22.0 6.9 %collective-permute-start.3 = (f32[1,1,256,256]{2,1,3,0:T(1,128)S(1)}, f32[1,1,256,256]{2,1,3,0:T(1,128)S(1)}, u32[]{:S(2)}, u32[]{:S(2)}) collective-permute-start(f32[1,1,256,256]{2,1,3,0:T(1,128)S(1)} %get-tuple-element.47), channel_id=1, source_target_pairs={{0,8},{8,16},{16,24},{24,32},{32,40},{40,48},{48,56},{56,64},{64,7... | collective-permute-start | bytes 786440 | tf_op jit(solution)/shard_map/ppermute | solution.py:19
  31.6 11.9 %collective-permute-start.4 = (f32[1,1,256,256]{2,1,3,0:T(1,128)S(1)}, f32[1,1,256,256]{2,1,3,0:T(1,128)S(1)}, u32[]{:S(2)}, u32[]{:S(2)}) collective-permute-start(f32[1,1,256,256]{2,1,3,0:T(1,128)S(1)} %get-tuple-element.44), channel_id=1, source_target_pairs={{8,0},{16,8},{24,16},{32,24},{40,32},{48,40},{56,48},{64,56},{72,6... | collective-permute-start | bytes 786440 | tf_op jit(solution)/shard_map/ppermute | solution.py:22
  33.5 10.0 %collective-permute-start.5 = (f32[1,1,256,256]{2,1,3,0:T(1,128)S(1)}, f32[1,1,256,256]{2,1,3,0:T(1,128)S(1)}, u32[]{:S(2)}, u32[]{:S(2)}) collective-permute-start(f32[1,1,256,256]{2,1,3,0:T(1,128)S(1)} %get-tuple-element.45), channel_id=1, source_target_pairs={{0,8},{8,16},{16,24},{24,32},{32,40},{40,48},{48,56},{56,64},{64,7... | collective-permute-start | bytes 786440 | tf_op jit(solution)/shard_map/ppermute | solution.py:19
  38.0 188.4 %collective-permute-start.6 = (f32[1,1,128,128]{3,2,1,0:T(8,128)S(1)}, f32[1,1,128,128]{3,2,1,0:T(8,128)S(1)}, u32[]{:S(2)}, u32[]{:S(2)}) collective-permute-start(f32[1,1,128,128]{3,2,1,0:T(8,128)S(1)} %broadcast.205), channel_id=1, source_target_pairs={{8,0},{16,8},{24,16},{32,24},{40,32},{48,40},{56,48},{64,56},{72,6... | collective-permute-start | bytes 196616 | tf_op jit(solution)/shard_map/ppermute | solution.py:22
  39.9 186.4 %collective-permute-start.7 = (f32[1,1,128,128]{3,2,1,0:T(8,128)S(1)}, f32[1,1,128,128]{3,2,1,0:T(8,128)S(1)}, u32[]{:S(2)}, u32[]{:S(2)}) collective-permute-start(f32[1,1,128,128]{3,2,1,0:T(8,128)S(1)} %broadcast.205), channel_id=1, source_target_pairs={{0,8},{8,16},{16,24},{24,32},{32,40},{40,48},{48,56},{56,64},{64,7... | collective-permute-start | bytes 196616 | tf_op jit(solution)/shard_map/ppermute | solution.py:19
  226.6 6.4 %collective-permute-start.8 = (f32[1,1,128,128]{3,2,1,0:T(8,128)S(1)}, f32[1,1,128,128]{3,2,1,0:T(8,128)S(1)}, u32[]{:S(2)}, u32[]{:S(2)}) collective-permute-start(f32[1,1,128,128]{3,2,1,0:T(8,128)S(1)} %get-tuple-element.56), channel_id=1, source_target_pairs={{8,0},{16,8},{24,16},{32,24},{40,32},{48,40},{56,48},{64,56},{72,6... | collective-permute-start | bytes 196616 | tf_op jit(solution)/shard_map/ppermute | solution.py:22
  234.5 13.0 %collective-permute-start.10 = (f32[1,1,128,128]{3,2,1,0:T(8,128)S(1)}, f32[1,1,128,128]{3,2,1,0:T(8,128)S(1)}, u32[]{:S(2)}, u32[]{:S(2)}) collective-permute-start(f32[1,1,128,128]{3,2,1,0:T(8,128)S(1)} %get-tuple-element.54), channel_id=1, source_target_pairs={{8,0},{16,8},{24,16},{32,24},{40,32},{48,40},{56,48},{64,56},{72,6... | collective-permute-start | bytes 196616 | tf_op jit(solution)/shard_map/ppermute | solution.py:22
  236.5 11.1 %collective-permute-start.11 = (f32[1,1,128,128]{3,2,1,0:T(8,128)S(1)}, f32[1,1,128,128]{3,2,1,0:T(8,128)S(1)}, u32[]{:S(2)}, u32[]{:S(2)}) collective-permute-start(f32[1,1,128,128]{3,2,1,0:T(8,128)S(1)} %get-tuple-element.55), channel_id=1, source_target_pairs={{0,8},{8,16},{16,24},{24,32},{32,40},{40,48},{48,56},{56,64},{64,7... | collective-permute-start | bytes 196616 | tf_op jit(solution)/shard_map/ppermute | solution.py:19
  240.8 32.1 %collective-permute-start.12 = (f32[1,1,64,64]{3,2,1,0:T(8,128)S(1)}, f32[1,1,64,64]{3,2,1,0:T(8,128)S(1)}, u32[]{:S(2)}, u32[]{:S(2)}) collective-permute-start(f32[1,1,64,64]{3,2,1,0:T(8,128)S(1)} %broadcast.210), channel_id=1, source_target_pairs={{8,0},{16,8},{24,16},{32,24},{40,32},{48,40},{56,48},{64,56},{72,6... | collective-permute-start | bytes 49160 | tf_op jit(solution)/shard_map/ppermute | solution.py:22
  242.7 30.2 %collective-permute-start.13 = (f32[1,1,64,64]{3,2,1,0:T(8,128)S(1)}, f32[1,1,64,64]{3,2,1,0:T(8,128)S(1)}, u32[]{:S(2)}, u32[]{:S(2)}) collective-permute-start(f32[1,1,64,64]{3,2,1,0:T(8,128)S(1)} %broadcast.210), channel_id=1, source_target_pairs={{0,8},{8,16},{16,24},{24,32},{32,40},{40,48},{48,56},{56,64},{64,7... | collective-permute-start | bytes 49160 | tf_op jit(solution)/shard_map/ppermute | solution.py:19
  273.0 7.1 %collective-permute-start.14 = (f32[1,1,64,64]{3,2,1,0:T(8,128)S(1)}, f32[1,1,64,64]{3,2,1,0:T(8,128)S(1)}, u32[]{:S(2)}, u32[]{:S(2)}) collective-permute-start(f32[1,1,64,64]{3,2,1,0:T(8,128)S(1)} %get-tuple-element.64), channel_id=1, source_target_pairs={{8,0},{16,8},{24,16},{32,24},{40,32},{48,40},{56,48},{64,56},{72,6... | collective-permute-start | bytes 49160 | tf_op jit(solution)/shard_map/ppermute | solution.py:22
  281.3 6.5 %collective-permute-start.16 = (f32[1,1,64,64]{3,2,1,0:T(8,128)S(1)}, f32[1,1,64,64]{3,2,1,0:T(8,128)S(1)}, u32[]{:S(2)}, u32[]{:S(2)}) collective-permute-start(f32[1,1,64,64]{3,2,1,0:T(8,128)S(1)} %get-tuple-element.62), channel_id=1, source_target_pairs={{8,0},{16,8},{24,16},{32,24},{40,32},{48,40},{56,48},{64,56},{72,6... | collective-permute-start | bytes 49160 | tf_op jit(solution)/shard_map/ppermute | solution.py:22
  292.2 17.6 %all-to-all-start = ((f32[16,1,1024]{2,1,0:T(1,128)}), f32[16,1,1024]{2,1,0:T(1,128)S(1)}, u32[]{:S(2)}, u32[]{:S(2)}) async-start(f32[16,1,1024]{2,1,0:T(1,128)} %reshape.153), calls=%async_computation | async-start | bytes 131072 | tf_op jit(solution)/shard_map/all_to_all | solution.py:35
  348.6 8.3 %collective-permute-start.26 = (f32[1,1,256,256]{2,1,3,0:T(1,128)S(1)}, f32[1,1,256,256]{2,1,3,0:T(1,128)S(1)}, u32[]{:S(2)}, u32[]{:S(2)}) collective-permute-start(f32[1,1,256,256]{2,1,3,0:T(1,128)S(1)} %get-tuple-element.42), channel_id=1, source_target_pairs={{8,0},{16,8},{24,16},{32,24},{40,32},{48,40},{56,48},{64,56},{72,6... | collective-permute-start | bytes 786440 | tf_op jit(solution)/shard_map/ppermute | solution.py:22
  350.5 7.6 %collective-permute-start.27 = (f32[1,1,256,256]{2,1,3,0:T(1,128)S(1)}, f32[1,1,256,256]{2,1,3,0:T(1,128)S(1)}, u32[]{:S(2)}, u32[]{:S(2)}) collective-permute-start(f32[1,1,256,256]{2,1,3,0:T(1,128)S(1)} %get-tuple-element.43), channel_id=1, source_target_pairs={{0,8},{8,16},{16,24},{24,32},{32,40},{40,48},{48,56},{56,64},{64,7... | collective-permute-start | bytes 786440 | tf_op jit(solution)/shard_map/ppermute | solution.py:19
  360.6 8.4 %collective-permute-start.28 = (f32[1,1,256,256]{2,1,3,0:T(1,128)S(1)}, f32[1,1,256,256]{2,1,3,0:T(1,128)S(1)}, u32[]{:S(2)}, u32[]{:S(2)}) collective-permute-start(f32[1,1,256,256]{2,1,3,0:T(1,128)S(1)} %get-tuple-element.40), channel_id=1, source_target_pairs={{8,0},{16,8},{24,16},{32,24},{40,32},{48,40},{56,48},{64,56},{72,6... | collective-permute-start | bytes 786440 | tf_op jit(solution)/shard_map/ppermute | solution.py:22
  362.5 7.7 %collective-permute-start.29 = (f32[1,1,256,256]{2,1,3,0:T(1,128)S(1)}, f32[1,1,256,256]{2,1,3,0:T(1,128)S(1)}, u32[]{:S(2)}, u32[]{:S(2)}) collective-permute-start(f32[1,1,256,256]{2,1,3,0:T(1,128)S(1)} %get-tuple-element.41), channel_id=1, source_target_pairs={{0,8},{8,16},{16,24},{24,32},{32,40},{40,48},{48,56},{56,64},{64,7... | collective-permute-start | bytes 786440 | tf_op jit(solution)/shard_map/ppermute | solution.py:19
  372.7 8.4 %collective-permute-start.30 = (f32[1,1,256,256]{2,1,3,0:T(1,128)S(1)}, f32[1,1,256,256]{2,1,3,0:T(1,128)S(1)}, u32[]{:S(2)}, u32[]{:S(2)}) collective-permute-start(f32[1,1,256,256]{2,1,3,0:T(1,128)S(1)} %get-tuple-element.38), channel_id=1, source_target_pairs={{8,0},{16,8},{24,16},{32,24},{40,32},{48,40},{56,48},{64,56},{72,6... | collective-permute-start | bytes 786440 | tf_op jit(solution)/shard_map/ppermute | solution.py:22
  374.7 7.7 %collective-permute-start.31 = (f32[1,1,256,256]{2,1,3,0:T(1,128)S(1)}, f32[1,1,256,256]{2,1,3,0:T(1,128)S(1)}, u32[]{:S(2)}, u32[]{:S(2)}) collective-permute-start(f32[1,1,256,256]{2,1,3,0:T(1,128)S(1)} %get-tuple-element.39), channel_id=1, source_target_pairs={{0,8},{8,16},{16,24},{24,32},{32,40},{40,48},{48,56},{56,64},{64,7... | collective-permute-start | bytes 786440 | tf_op jit(solution)/shard_map/ppermute | solution.py:19
  387.3 16.7 %all-to-all-start.1 = ((f32[16,1,2]{2,1,0:T(1,128)}), f32[16,1,2]{2,1,0:T(1,128)S(1)}, u32[]{:S(2)}, u32[]{:S(2)}) async-start(f32[16,1,2]{2,1,0:T(1,128)} %broadcast_in_dim.88), calls=%async_computation.1 | async-start | bytes 16384 | tf_op jit(solution)/shard_map/all_to_all | solution.py:35
  405.9 12.9 %all-to-all-start.2 = ((f32[8,1,1]{2,1,0:T(1,128)}), f32[8,1,1]{2,1,0:T(1,128)S(1)}, u32[]{:S(2)}, u32[]{:S(2)}) async-start(f32[8,1,1]{2,1,0:T(1,128)} %broadcast_in_dim.89), calls=%async_computation.2 | async-start | bytes 8192 | tf_op jit(solution)/shard_map/all_to_all | solution.py:35
  (15 other events, 115.2 us)
where the time goes:
time: 423 us; the launch traced here: 421 us
  local copies, waits for them, and re-layouts  177 us (42%)
  starting transfers between devices  129 us (30%)
  other arithmetic  72 us (17%)
  waiting for transfers between devices  34.5 us (8%)
  between operations  8.58 us (2%)
    reshape x2, local copies, waits for them, and re-layouts, restrict(): field.reshape(pairs, zsize // 2, 2, ysize // 2, 2, xsize // 2, 2)  154 us
    ppermute x16, starting transfers between devices, with_halo(): lax.ppermute(lax.slice_in_dim(block, block.shape[dim] - width, None, axis...  67 us
    reduce_sum x4, other arithmetic, restrict(): field.reshape(pairs, zsize // 2, 2, ysize // 2, 2, xsize // 2, 2)  48.5 us
    ppermute x16, starting transfers between devices, with_halo(): lax.ppermute(lax.slice_in_dim(block, 0, width, axis=dim), axis, backward)  32.5 us
    all_to_all x3, starting transfers between devices, copy_for_each(): lax.all_to_all(jnp.broadcast_to(array[None], (peers, *array.shape)), axis...  29.3 us
    all_to_all x3, waiting for transfers between devices, copy_for_each(): lax.all_to_all(jnp.broadcast_to(array[None], (peers, *array.shape)), axis...  13.6 us
    ppermute x16, waiting for transfers between devices, with_halo(): lax.ppermute(lax.slice_in_dim(block, block.shape[dim] - width, None, axis...  12.4 us
    ppermute x16, waiting for transfers between devices, with_halo(): lax.ppermute(lax.slice_in_dim(block, 0, width, axis=dim), axis, backward)  8.49 us
  transfers between devices with their start and end apart: 35, of which 18 were waited for; matrix products, arithmetic and copies ran while one was open for 51% of the time, Pallas kernels for 0%

commit v1 on v0

v1 whole, which is shorter than its diff:
```python
import functools

import jax
import jax.numpy as jnp
from jax import lax
from jax.experimental import pallas as pl
from jax.experimental.pallas import tpu as pltpu
from jax.sharding import PartitionSpec as P

MESH = pl.DeviceIdType.MESH
F32, BF16 = jnp.float32, jnp.bfloat16
PAD = 8
CH = 32
NINTH = 1.0 / 9.0
N81 = 1.0 / 81.0


def lane_iota(shape):
    return lax.broadcasted_iota(jnp.int32, shape, len(shape) - 1)


def roll(x, shift):
    return pltpu.roll(x, shift % x.shape[-1], x.ndim - 1)


def from_left(x, width=128):
    return jnp.where(lane_iota(x.shape) % width == 0, 0.0, roll(x, 1))


def from_right(x, width=128):
    return jnp.where(lane_iota(x.shape) % width == width - 1, 0.0, roll(x, -1))


def split_dot(x, m):
    hi = x.astype(BF16)
    rest = x - hi.astype(F32)
    mid = rest.astype(BF16)
    low = (rest - mid.astype(F32)).astype(BF16)
    dot = functools.partial(jnp.dot, preferred_element_type=F32)
    return dot(hi, m) + dot(mid, m) + dot(low, m)


def selection(shape, test):
    a = lax.broadcasted_iota(jnp.int32, shape, 0)
    b = lax.broadcasted_iota(jnp.int32, shape, 1)
    return jnp.where(test(a, b), 1.0, 0.0).astype(BF16)


def fold(x):
    return x.reshape(x.shape[0] // 8, 8, x.shape[1]).sum(axis=0)


def rows(ref, z, ph, r, n, dr=0):
    return ref[z, ph, pl.ds(PAD + r + dr, n), :]


def nbxy0(ref, z, r, n, c):
    out = []
    for yp in range(2):
        for xp in range(2):
            side = c[2 * yp + 1 - xp]
            x = side + (from_right(side) if xp else from_left(side))
            other = 2 * (1 - yp) + xp
            y = c[other] + rows(ref, z, other, r, n, 1 if yp else -1)
            out.append(x + y)
    return out


def phase_sums(ref, z, r, n, c):
    total = (c[0] + c[1]) + (c[2] + c[3])
    shifts = from_left(c[1] + c[3]) + from_right(c[0] + c[2])
    shifts = shifts + (rows(ref, z, 2, r, n, -1) + rows(ref, z, 3, r, n, -1))
    shifts = shifts + (rows(ref, z, 0, r, n, 1) + rows(ref, z, 1, r, n, 1))
    return total, shifts


def center(ref, z, r, n):
    return [rows(ref, z, ph, r, n) for ph in range(4)]


def crow(ref, z, r, n, dr=0):
    return ref[z, pl.ds(PAD + r + dr, n), :]


def nbxy(ref, z, r, n, c, width):
    y = crow(ref, z, r, n, -1) + crow(ref, z, r, n, 1)
    return y + (from_left(c, width) + from_right(c, width))


def kernel(
    gz, pairs,
    pidx, pweight, orbitals, pot, res_out, en_out,
    orb0, orb1, orb2, orb3, orb4, orb5, orb6, orb7, px, tmp, f, a, b, g0, g0o, s1, a1, b1, t1, g1, g1o, pe1,
    s2, a2, b2, t2, pe2, t3, s3, a3, b3, sums, ens, obuf,
    orb_sem, fs, fr, g0s, g0r, h1s, h1r, g1s, g1r, h2s, h2r, t3s, t3r, ss, sr, es, er, out_sem,
):
    d = lax.axis_index("gz")
    me = lax.axis_index("pair")
    has_lo, has_hi = d > 0, d < gz - 1
    flo, fhi = has_lo.astype(F32), has_hi.astype(F32)

    def remote(src, dst, s_sem, r_sem, **to):
        return pltpu.make_async_remote_copy(
            src_ref=src, dst_ref=dst, send_sem=s_sem, recv_sem=r_sem, device_id=to, device_id_type=MESH
        )

    orb = (orb0, orb1, orb2, orb3, orb4, orb5, orb6, orb7)

    def orb_copy(z):
        return pltpu.make_async_copy(orbitals.at[:, z], orb[z], orb_sem.at[z])

    for z in (0, 7, 1, 6, 2, 5, 3, 4):
        orb_copy(z).start()
    barrier = pltpu.get_barrier_semaphore()

    @pl.loop(1, gz)
    def _(o):
        pl.semaphore_signal(barrier, inc=1, device_id={"gz": lax.rem(d + o, gz)}, device_id_type=MESH)

    @pl.loop(1, pairs)
    def _(o):
        pl.semaphore_signal(barrier, inc=1, device_id={"pair": lax.rem(me + o, pairs)}, device_id_type=MESH)

    px[...] = selection((256, 256), lambda i, j: j == (i & 1) * 128 + (i >> 1))
    pad0 = jnp.zeros((4, PAD, 128), F32)

    @pl.loop(0, 16)
    def _(z):
        for ref in (f, a, b):
            ref[z, :, pl.ds(0, PAD), :] = pad0
            ref[z, :, pl.ds(PAD + 128, PAD), :] = pad0

    def clear_outside(first):
        @pl.loop(first, first + 4)
        def _(z):
            for ref in (f, a, b):
                for ph in range(4):
                    ref[z, ph, pl.ds(PAD, 128), :] = jnp.zeros((128, 128), F32)

        @pl.when(first == 0)
        def _():
            @pl.loop(0, 5)
            def _(z):
                s1[z, pl.ds(PAD, 128), :] = jnp.zeros((128, 128), F32)

        @pl.when(first > 0)
        def _():
            @pl.loop(9, 14)
            def _(z):
                s1[z, pl.ds(PAD, 128), :] = jnp.zeros((128, 128), F32)

    @pl.when(d == 0)
    def _():
        clear_outside(0)
        g0[0] = jnp.zeros((128, 128), F32)
        g1[0] = jnp.zeros((64, 128), F32)

    @pl.when(d == gz - 1)
    def _():
        clear_outside(12)
        g0[1] = jnp.zeros((128, 128), F32)
        g1[1] = jnp.zeros((64, 128), F32)

    @pl.when(d == 1)
    def _():
        s1[0, pl.ds(PAD, 128), :] = jnp.zeros((128, 128), F32)

    @pl.when(d == gz - 2)
    def _():
        s1[13, pl.ds(PAD, 128), :] = jnp.zeros((128, 128), F32)

    @pl.loop(0, 14)
    def _(z):
        s1[z, pl.ds(0, PAD), :] = jnp.zeros((PAD, 128), F32)
        s1[z, pl.ds(PAD + 128, PAD), :] = jnp.zeros((PAD, 128), F32)
        a1[z] = jnp.zeros((144, 128), F32)
        b1[z] = jnp.zeros((144, 128), F32)

    @pl.loop(0, 7)
    def _(p):
        s2[p, pl.ds(0, PAD), :] = jnp.zeros((PAD, 128), F32)
        s2[p, pl.ds(PAD + 64, PAD), :] = jnp.zeros((PAD, 128), F32)
        a2[p] = jnp.zeros((80, 128), F32)
        b2[p] = jnp.zeros((80, 128), F32)
        at = d + p - 3

        @pl.when(jnp.logical_or(at < 0, at >= gz))
        def _():
            s2[p, pl.ds(PAD, 64), :] = jnp.zeros((64, 128), F32)

    for q in range(4):
        a3[q] = jnp.zeros((48, 128), F32)
        b3[q] = jnp.zeros((48, 128), F32)

    i0, i1 = pidx[0, 0], pidx[0, 1]

    for i, z in enumerate((0, 7, 1, 6, 2, 5, 3, 4)):
        orb_copy(z).wait()
        slot = i % 2
        left = jnp.dot(orb[z][i0], px[...], preferred_element_type=F32)
        right = jnp.dot(orb[z][i1], px[...], preferred_element_type=F32)
        both = left * right
        tmp[slot, 0] = both[:, :128]
        tmp[slot, 1] = both[:, 128:]
        for yp in range(2):
            for xp in range(2):
                f[z + 4, 2 * yp + xp, pl.ds(PAD, 128), :] = tmp[slot, xp, pl.ds(yp, 128, stride=2), :]

    def w_plane(z, lo, hi):
        for r in range(0, 128, CH):
            c = center(f, z, r, CH)
            nb = nbxy0(f, z, r, CH, c)
            for ph in range(4):
                t = 12.0 * c[ph] + nb[ph]
                if lo:
                    t = t + rows(f, z - 1, ph, r, CH)
                if hi:
                    t = t + rows(f, z + 1, ph, r, CH)
                a[z, ph, pl.ds(PAD + r, CH), :] = t

    w_plane(4, False, True)
    w_plane(11, True, False)

    pl.semaphore_wait(barrier, gz - 1 + pairs - 1)

    for side, z in ((0, 4), (1, 11)):
        for r in range(0, 128, CH):
            total, shifts = phase_sums(f, z, r, CH, center(f, z, r, CH))
            w = center(a, z, r, CH)
            g0o[side, pl.ds(r, CH), :] = (0.5 * N81) * (
                shifts - 3.0 * total + ((w[0] + w[1]) + (w[2] + w[3]))
            )

    def exchange(out, landed, s_sems, r_sems):
        lo = remote(out.at[0], landed.at[1], s_sems.at[0], r_sems.at[1], gz=jnp.maximum(d - 1, 0))
        hi = remote(out.at[1], landed.at[0], s_sems.at[1], r_sems.at[0], gz=jnp.minimum(d + 1, gz - 1))
        return lo, hi

    g0_lo, g0_hi = exchange(g0o, g0, g0s, g0r)

    @pl.when(has_lo)
    def _():
        g0_lo.start()

    @pl.when(has_hi)
    def _():
        g0_hi.start()

    def f_copy(side, k):
        if side == 0:
            return remote(
                f.at[4 + k, :, pl.ds(PAD, 128), :], f.at[12 + k, :, pl.ds(PAD, 128), :],
                fs.at[0, k], fr.at[1, k], gz=jnp.maximum(d - 1, 0),
            )
        return remote(
            f.at[8 + k, :, pl.ds(PAD, 128), :], f.at[k, :, pl.ds(PAD, 128), :],
            fs.at[1, k], fr.at[0, k], gz=jnp.minimum(d + 1, gz - 1),
        )

    def f_start(*which):
        @pl.when(has_lo)
        def _():
            for k in which:
                f_copy(0, k).start()

        @pl.when(has_hi)
        def _():
            for k in which:
                f_copy(1, 3 - k).start()

    f_start(0)

    @pl.loop(5, 11)
    def _(z):
        w_plane(z, True, True)

    for ph in range(4):
        a[3, ph, pl.ds(PAD, 128), :] = flo * f[4, ph, pl.ds(PAD, 128), :]
        a[12, ph, pl.ds(PAD, 128), :] = fhi * f[11, ph, pl.ds(PAD, 128), :]

    @pl.loop(0, 4)
    def _(j):
        for r in range(0, 128, CH):
            out = None
            for dz in range(2):
                z = 4 + 2 * j + dz
                c = center(a, z, r, CH)
                total, shifts = phase_sums(a, z, r, CH, c)
                below, above, src = center(a, z - 1, r, CH), center(a, z + 1, r, CH), center(f, z, r, CH)
                zs = ((below[0] + below[1]) + (below[2] + below[3])) + (
                    (above[0] + above[1]) + (above[2] + above[3])
                )
                q = ((src[0] + src[1]) + (src[2] + src[3])) + N81 * (zs - 4.0 * total + shifts)
                out = q if out is None else out + q
            s1[5 + j, pl.ds(PAD + r, CH), :] = 0.5 * out

    @pl.when(has_lo)
    def _():
        g0_hi.wait_recv()
        s1[5, pl.ds(PAD, 128), :] += g0[0]

    @pl.when(has_hi)
    def _():
        g0_lo.wait_recv()
        s1[8, pl.ds(PAD, 128), :] += g0[1]

    def w1_plane(z, lo, hi):
        for r in range(0, 128, 64):
            c = crow(s1, z, r, 64)
            t = 12.0 * c + nbxy(s1, z, r, 64, c, 128)
            if lo:
                t = t + crow(s1, z - 1, r, 64)
            if hi:
                t = t + crow(s1, z + 1, r, 64)
            a1[z, pl.ds(PAD + r, 64), :] = t

    for z in range(5, 9):
        w1_plane(z, z > 5, z < 8)
    a1[4, pl.ds(PAD, 128), :] = flo * crow(s1, 5, 0, 128)
    a1[9, pl.ds(PAD, 128), :] = fhi * crow(s1, 8, 0, 128)
    for slot, z in ((0, 5), (3, 8)):
        for r in range(0, 128, 64):
            c = crow(s1, z, r, 64)
            t1[slot, pl.ds(r, 64), :] = (0.5 * N81) * (
                nbxy(s1, z, r, 64, c, 128) - 5.0 * c + crow(a1, z, r, 64)
            )
    for slot in (1, 2):
        for r in range(0, 128, 64):
            out = None
            for z in (3 + 2 * slot, 4 + 2 * slot):
                c = crow(a1, z, r, 64)
                nb = nbxy(a1, z, r, 64, c, 128) + (crow(a1, z - 1, r, 64) + crow(a1, z + 1, r, 64))
                q = crow(s1, z, r, 64) + N81 * (nb - 6.0 * c)
                out = q if out is None else out + q
            t1[slot, pl.ds(r, 64), :] = 0.5 * out

    def ypair(ref, slot, n):
        return ref[slot, pl.ds(0, n, stride=2), :] + ref[slot, pl.ds(1, n, stride=2), :]

    m_first = selection((128, 128), lambda i, j: (i >> 1) == j)
    m_second = selection((128, 128), lambda i, j: (i >> 1) + 64 == j)
    g1o[0] = split_dot(ypair(t1, 0, 64), m_second)
    g1o[1] = split_dot(ypair(t1, 3, 64), m_first)
    g1_lo, g1_hi = exchange(g1o, g1, g1s, g1r)

    @pl.when(has_lo)
    def _():
        g1_lo.start()

    @pl.when(has_hi)
    def _():
        g1_hi.start()

    s2[3, pl.ds(PAD, 64), :] = split_dot(ypair(t1, 1, 64), m_first) + split_dot(ypair(t1, 2, 64), m_second)

    def h1_copy(i):
        here, there, step = ((5, 9, -1), (5, 1, 1), (5, 13, -2), (8, 0, 2))[i]
        n = 4 if abs(step) == 1 else 1
        to = jnp.clip(d + step, 0, gz - 1)
        return remote(
            s1.at[pl.ds(here, n), pl.ds(PAD, 128), :], s1.at[pl.ds(there, n), pl.ds(PAD, 128), :],
            h1s.at[i], h1r.at[i], gz=to,
        )

    h1_sends = [d >= 1, d <= gz - 2, d >= 2, d <= gz - 3]
    h1_recvs = [d <= gz - 2, d >= 1, d <= gz - 3, d >= 2]

    def h1_start():
        for i in range(4):
            @pl.when(h1_sends[i])
            def _():
                h1_copy(i).start()

    h1_start()

    @pl.when(has_lo)
    def _():
        g1_hi.wait_recv()
        s2[3, pl.ds(PAD, 64), :] += g1[0]

    @pl.when(has_hi)
    def _():
        g1_lo.wait_recv()
        s2[3, pl.ds(PAD, 64), :] += g1[1]

    low_half = lane_iota((64, 128)) < 64

    def nb2(ref, p, c):
        z = roll(c + jnp.where(low_half, crow(ref, p + 1, 0, 64), crow(ref, p - 1, 0, 64)), 64)
        return nbxy(ref, p, 0, 64, c, 64) + z

    def h2_copy(i):
        step = (-3, -2, -1, 1, 2, 3)[i]
        to = jnp.clip(d + step, 0, gz - 1)
        return remote(
            s2.at[3, pl.ds(PAD, 64), :], s2.at[3 - step, pl.ds(PAD, 64), :], h2s.at[i], h2r.at[i], gz=to
        )

    def inside(step):
        at = d + step
        return jnp.logical_and(at >= 0, at < gz)

    c = crow(s2, 3, 0, 64)
    turned = roll(c, 64)
    w0 = 12.0 * c + nbxy(s2, 3, 0, 64, c, 64) + turned
    a2[3, pl.ds(PAD, 64), :] = w0
    a2[2, pl.ds(PAD, 64), :] = flo * jnp.where(low_half, 0.0, turned)
    a2[4, pl.ds(PAD, 64), :] = fhi * jnp.where(low_half, turned, 0.0)
    for p in (2, 3, 4):
        w = crow(a2, p, 0, 64)
        r = N81 * (nb2(a2, p, w) - 6.0 * w)
        t2[p - 2] = r + c if p == 3 else r
    tile = None
    for p in range(3):
        block = lax.rem(d + p - 1 + gz, 4) * 32
        m = selection((128, 128), lambda i, j: ((i & 63) >> 1) + block == j)
        part = split_dot(ypair(t2, p, 32), m)
        tile = part if tile is None else tile + part
    t3[d] = 0.5 * tile

    def t3_copy(o):
        to = lax.rem(d + o, gz)
        return remote(t3.at[d], t3.at[d], t3s.at[o], t3r.at[d], gz=to)

    @pl.loop(1, gz)
    def _(o):
        t3_copy(o).start()

    for i, step in enumerate((-3, -2, -1, 1, 2, 3)):
        @pl.when(inside(step))
        def _():
            h2_copy(i).start()

    f_start(1, 2, 3)

    @pl.loop(1, gz)
    def _(o):
        peer = lax.rem(d + o, gz)
        remote(t3.at[peer], t3.at[peer], t3s.at[o], t3r.at[peer], gz=peer).wait_recv()

    lane32 = lane_iota((32, 128))
    for q in range(4):
        total = None
        for e in range(max(4 * q - 1, 0), min(4 * q + 5, gz)):
            x = t3[e]
            if e == 4 * q - 1:
                x = jnp.where(lane32 < 32, x, 0.0)
            elif e == 4 * q + 4:
                x = jnp.where(lane32 >= 96, x, 0.0)
            elif e == 4 * q:
                x = jnp.where(lane32 < 96, x, 0.0)
            elif e == 4 * q + 3:
                x = jnp.where(lane32 >= 32, x, 0.0)
            total = x if total is None else total + x
        s3[q] = total * NINTH
        a3[q, pl.ds(PAD, 32), :] = total * NINTH

    def sweep3(src, dst):
        v = [crow(src, q, 0, 32) for q in range(4)]
        for q in range(4):
            after = v[q + 1] if q < 3 else jnp.zeros_like(v[0])
            before = v[q - 1] if q > 0 else jnp.zeros_like(v[0])
            nz = roll(jnp.where(lane32 < 32, after, v[q]), -32)
            nz = nz + roll(jnp.where(lane32 >= 96, before, v[q]), 32)
            nb = nbxy(src, q, 0, 32, v[q], 32) + nz
            dst[q, pl.ds(PAD, 32), :] = (1.0 / 3.0) * v[q] + (NINTH * nb + s3[q])

    @pl.loop(0, 3)
    def _(i):
        sweep3(a3, b3)
        sweep3(b3, a3)

    sweep3(a3, b3)

    for i, step in enumerate((-3, -2, -1, 1, 2, 3)):
        @pl.when(inside(-step))
        def _():
            h2_copy(i).wait_recv()

    flag2 = {p: inside(p - 3).astype(F32) for p in range(1, 6)}
    for p in range(1, 6):
        at = d + p - 3
        q = jnp.clip(at // 4, 0, 3)
        block = lax.rem(at + gz, 4) * 32
        m = selection((128, 128), lambda i, j: i == ((j & 63) >> 1) + block)
        e = split_dot(b3[q, pl.ds(PAD, 32), :], m)
        pe2[p - 1, pl.ds(0, 32, stride=2), :] = e
        pe2[p - 1, pl.ds(1, 32, stride=2), :] = e
    for p in range(1, 6):
        c = crow(s2, p, 0, 64)
        w = 12.0 * c + nb2(s2, p, c)
        a2[p, pl.ds(PAD, 64), :] = flag2[p] * (N81 * w + pe2[p - 1])

    def sweep2(src, dst, p):
        c = crow(src, p, 0, 64)
        dst[p, pl.ds(PAD, 64), :] = flag2[p] * (
            (1.0 / 3.0) * c + NINTH * (nb2(src, p, c) + crow(s2, p, 0, 64))
        )

    for p in range(1, 6):
        sweep2(a2, b2, p)
    for p in range(2, 5):
        sweep2(b2, a2, p)

    for i in range(4):
        @pl.when(h1_recvs[i])
        def _():
            h1_copy(i).wait_recv()

    for half in range(2):
        m = selection((128, 128), lambda i, j: i == (j >> 1) + 64 * half)
        for p in range(3):
            e = split_dot(a2[2 + p, pl.ds(PAD, 64), :], m)
            pe1[2 * p + half, pl.ds(0, 64, stride=2), :] = e
            pe1[2 * p + half, pl.ds(1, 64, stride=2), :] = e

    def bounds(first, last, own):
        return jnp.where(has_lo, first, 0), jnp.where(has_hi, last + 1, own)

    lo1, hi1 = bounds(-4, 7, 4)

    @pl.loop(lo1 + 5, hi1 + 5)
    def _(z):
        for r in range(0, 128, 64):
            c = crow(s1, z, r, 64)
            w = 12.0 * c + nbxy(s1, z, r, 64, c, 128) + (crow(s1, z - 1, r, 64) + crow(s1, z + 1, r, 64))
            a1[z, pl.ds(PAD + r, 64), :] = N81 * w + pe1[(z - 1) // 2, pl.ds(r, 64), :]

    def sweep1(src, dst, first, last):
        lo, hi = bounds(first, last, 4)

        @pl.loop(lo + 5, hi + 5)
        def _(z):
            for r in range(0, 128, 64):
                c = crow(src, z, r, 64)
                nb = nbxy(src, z, r, 64, c, 128) + (crow(src, z - 1, r, 64) + crow(src, z + 1, r, 64))
                dst[z, pl.ds(PAD + r, 64), :] = (1.0 / 3.0) * c + NINTH * (nb + crow(s1, z, r, 64))

    sweep1(a1, b1, -3, 6)
    sweep1(b1, a1, -2, 5)

    @pl.when(has_lo)
    def _():
        for k in range(4):
            f_copy(1, k).wait_recv()

    @pl.when(has_hi)
    def _():
        for k in range(4):
            f_copy(0, k).wait_recv()

    lo0, hi0 = bounds(-3, 10, 8)

    @pl.loop(lo0 + 4, 5)
    def _(z):
        w_plane(z, True, True)

    @pl.loop(11, hi0 + 4)
    def _(z):
        w_plane(z, True, True)

    @pl.loop(lo0 + 4, hi0 + 4)
    def _(z):
        e = a1[z // 2 + 3, pl.ds(PAD, 128), :]
        for ph in range(4):
            a[z, ph, pl.ds(PAD, 128), :] = N81 * a[z, ph, pl.ds(PAD, 128), :] + e

    def sweep0(src, dst, first, last):
        lo, hi = bounds(first, last, 8)

        @pl.loop(lo + 4, hi + 4)
        def _(z):
            for r in range(0, 128, CH):
                c = center(src, z, r, CH)
                nb = nbxy0(src, z, r, CH, c)
                for ph in range(4):
                    t = nb[ph] + (rows(src, z - 1, ph, r, CH) + rows(src, z + 1, ph, r, CH))
                    t = t + rows(f, z, ph, r, CH)
                    dst[z, ph, pl.ds(PAD + r, CH), :] = (1.0 / 3.0) * c[ph] + NINTH * t

    sweep0(a, b, -2, 9)
    sweep0(b, a, -1, 8)

    def final(z, carry):
        squares, products = carry
        for r in range(0, 128, CH):
            c = center(a, z, r, CH)
            nb = nbxy0(a, z, r, CH, c)
            for ph in range(4):
                t = nb[ph] + (rows(a, z - 1, ph, r, CH) + rows(a, z + 1, ph, r, CH))
                src = rows(f, z, ph, r, CH)
                left = (src - 6.0 * c[ph]) + t
                squares = squares + fold(left * left)
                products = products + fold(src * c[ph])
        return squares, products

    zero = jnp.zeros((8, 128), F32)
    squares, products = lax.fori_loop(4, 12, final, (zero, zero))
    sums[d, pl.ds(0, 8), :] = squares
    sums[d, pl.ds(8, 8), :] = products

    @pl.loop(1, gz)
    def _(o):
        remote(sums.at[d], sums.at[d], ss.at[o], sr.at[d], gz=lax.rem(d + o, gz)).start()

    px[...] = selection((256, 256), lambda i, j: i == (j & 1) * 128 + (j >> 1))

    def out_copy(z, half):
        return pltpu.make_async_copy(
            obuf.at[z, half], pot.at[0, z, :, pl.ds(128 * half, 128)], out_sem.at[z, half]
        )

    @pl.loop(0, 8)
    def _(z):
        for yp in range(2):
            x = jnp.concatenate(
                [a[z + 4, 2 * yp, pl.ds(PAD, 128), :], a[z + 4, 2 * yp + 1, pl.ds(PAD, 128), :]], axis=1
            )
            y = split_dot(x, px[...])
            for half in range(2):
                obuf[z, half, pl.ds(yp, 128, stride=2), :] = y[:, 128 * half:128 * half + 128]
        for half in range(2):
            out_copy(z, half).start()

    @pl.loop(1, gz)
    def _(o):
        peer = lax.rem(d + o, gz)
        remote(sums.at[peer], sums.at[peer], ss.at[o], sr.at[peer], gz=peer).wait_recv()

    total = sums[0]
    for e in range(1, gz):
        total = total + sums[e]
    cells = 1.0 / (gz * 8 * 256 * 256)
    ens[me] = pweight[0] * total[8:]

    @pl.loop(1, pairs)
    def _(o):
        remote(ens.at[me], ens.at[me], es.at[o], er.at[me], pair=lax.rem(me + o, pairs)).start()

    norm = jnp.sqrt(jnp.full((8, 128), jnp.sum(total[:8]) * cells, F32))
    res_out[0] = jnp.max(norm)

    @pl.loop(1, pairs)
    def _(o):
        peer = lax.rem(me + o, pairs)
        remote(ens.at[peer], ens.at[peer], es.at[o], er.at[peer], pair=peer).wait_recv()

    energy = ens[0]
    for e in range(1, pairs):
        energy = energy + ens[e]
    en_out[0] = jnp.sum(energy) * (-0.5 * cells)

    for cond, side in ((has_lo, 0), (has_hi, 1)):
        @pl.when(cond)
        def _():
            (g0_lo, g0_hi)[side].wait_send()
            (g1_lo, g1_hi)[side].wait_send()
            for k in range(4):
                f_copy(side, k).wait_send()

    for i in range(4):
        @pl.when(h1_sends[i])
        def _():
            h1_copy(i).wait_send()

    for i, step in enumerate((-3, -2, -1, 1, 2, 3)):
        @pl.when(inside(step))
        def _():
            h2_copy(i).wait_send()

    @pl.loop(1, gz)
    def _(o):
        t3_copy(o).wait_send()
        remote(sums.at[d], sums.at[d], ss.at[o], sr.at[d], gz=lax.rem(d + o, gz)).wait_send()

    @pl.loop(1, pairs)
    def _(o):
        remote(ens.at[me], ens.at[me], es.at[o], er.at[me], pair=lax.rem(me + o, pairs)).wait_send()

    @pl.loop(0, 8)
    def _(z):
        for half in range(2):
            out_copy(z, half).wait()


def solution(mesh):
    gz, pairs = mesh.shape["gz"], mesh.shape["pair"]
    dma, vmem = pltpu.SemaphoreType.DMA, pltpu.VMEM
    field = vmem((16, 4, 144, 128), F32)
    level1, level2, level3 = vmem((14, 144, 128), F32), vmem((7, 80, 128), F32), vmem((4, 48, 128), F32)

    def per_device(orbitals, pair_index, pair_weight):
        return pl.pallas_call(
            functools.partial(kernel, gz, pairs),
            out_shape=(
                jax.ShapeDtypeStruct((1, 8, 256, 256), F32),
                jax.ShapeDtypeStruct((1,), F32),
                jax.ShapeDtypeStruct((1,), F32),
            ),
            in_specs=[
                pl.BlockSpec(memory_space=pltpu.SMEM),
                pl.BlockSpec(memory_space=pltpu.SMEM),
                pl.BlockSpec(memory_space=pl.ANY),
            ],
            out_specs=(
                pl.BlockSpec(memory_space=pl.ANY),
                pl.BlockSpec(memory_space=pltpu.SMEM),
                pl.BlockSpec(memory_space=pltpu.SMEM),
            ),
            scratch_shapes=[
                *[vmem((8, 256, 256), BF16)] * 8,
                vmem((256, 256), BF16),
                vmem((2, 2, 256, 128), F32),
                field, field, field,
                vmem((2, 128, 128), F32), vmem((2, 128, 128), F32),
                level1, level1, level1,
                vmem((4, 128, 128), F32),
                vmem((2, 64, 128), F32), vmem((2, 64, 128), F32),
                vmem((6, 128, 128), F32),
                level2, level2, level2,
                vmem((3, 64, 128), F32),
                vmem((5, 64, 128), F32),
                vmem((gz, 32, 128), F32),
                vmem((4, 32, 128), F32),
                level3, level3,
                vmem((gz, 16, 128), F32),
                vmem((pairs, 8, 128), F32),
                vmem((8, 2, 256, 128), F32),
                dma((8,)),
                dma((2, 4)), dma((2, 4)),
                dma((2,)), dma((2,)),
                dma((4,)), dma((4,)),
                dma((2,)), dma((2,)),
                dma((6,)), dma((6,)),
                dma((gz,)), dma((gz,)),
                dma((gz,)), dma((gz,)),
                dma((pairs,)), dma((pairs,)),
                dma((8, 2)),
            ],
            compiler_params=pltpu.CompilerParams(
                collective_id=0, has_side_effects=True, vmem_limit_bytes=60 * 1024 * 1024
            ),
            name="vcycle",
        )(pair_index, pair_weight, orbitals)

    return jax.shard_map(
        per_device,
        mesh=mesh,
        in_specs=(P(None, "gz", None, None), P("pair", None), P("pair")),
        out_specs=(P("pair", "gz", None, None), P("pair"), P()),
        check_vma=False,
    )
```

time: 423 us -> 75.9 us (0.18)
  local copies, waits for them, and re-layouts: 177 us -> 3.05 us
  starting transfers between devices: 129 us -> 0 us
  other arithmetic: 72 us -> 0 us
  Pallas kernels: 0 us -> 67.9 us
  waiting for transfers between devices: 34.5 us -> 0 us
    reshape x2 -> x0, local copies, waits for them, and re-layouts: 154 us -> none  [restrict(): field.reshape(pairs, zsize // 2, 2, ysize // 2, 2, xsize // 2, 2)]
    ppermute x32 -> x0, starting transfers between devices: 99.5 us -> none  [the longest x16 67 us: with_halo(): lax.ppermute(lax.slice_in_dim(block, block.shape[dim] - width, None, axis...]
    pallas_call x0 -> x1, Pallas kernels: none -> 67.9 us  [per_device(): pl.pallas_call(functools.partial(kernel, gz, pairs), out_shape=(jax.Shape...]
    reduce_sum x7 -> x0, other arithmetic: 52.1 us -> none  [the longest x4 48.5 us: restrict(): field.reshape(pairs, zsize // 2, 2, ysize // 2, 2, xsize // 2, 2)]
    all_to_all x3 -> x0, starting transfers between devices: 29.3 us -> none  [copy_for_each(): lax.all_to_all(jnp.broadcast_to(array[None], (peers, *array.shape)), axis...]
    ppermute x32 -> x0, waiting for transfers between devices: 20.9 us -> none  [the longest x16 12.4 us: with_halo(): lax.ppermute(lax.slice_in_dim(block, block.shape[dim] - width, None, axis...]
    all_to_all x3 -> x0, waiting for transfers between devices: 13.6 us -> none  [copy_for_each(): lax.all_to_all(jnp.broadcast_to(array[None], (peers, *array.shape)), axis...]
    add x19 -> x0, other arithmetic: 11.2 us -> none  [the longest x9 7.67 us: sweep(): field + (source - apply_op(field, level)) * (relax * 4.0 ** level / 6.0)]
  transfers between devices with their start and end apart: 35 -> 0, of which waited for: 18 -> 0; matrix products, arithmetic and copies ran while one was open for 51% -> 0% of each run, Pallas kernels for 0% -> 0%
where the time goes in v1:
time: 75.9 us; the launch traced here: 75.7 us
  Pallas kernels  67.9 us (89%)
  between operations  4.77 us (6%)
  local copies, waits for them, and re-layouts  3.05 us (4%)
    pallas_call x1, Pallas kernels, per_device(): pl.pallas_call(functools.partial(kernel, gz, pairs), out_shape=(jax.Shape...  67.9 us
    unnamed x1, local copies, waits for them, and re-layouts  3.05 us

profile of v1, /device:TPU:1, one launch (start us, length us, event | category | flops | bytes accessed | tf_op | source)
XLA Modules:
  0.0 75.7 jit_solution(17340676033164219394)
XLA Ops:
  1.3 67.9 %vcycle.1 = (f32[1,8,256,256]{3,2,1,0:T(8,128)}, f32[1]{0:T(128)}, f32[1]{0:T(128)}) custom-call(s32[1,2]{1,0:T(1,128)} %pidx.1, f32[1]{0:T(128)S(6)} %copy.9.pweight, bf16[8,8,256,256]{3,2,1,0:T(8,128)(2,1)} %orbitals.1), custom_call_target="tpu_custom_call" | custom-call | tf_op jit(solution)/shard_map/vcycle/pallas_call | solution.py:693
  69.2 3.0 %copy.10 = f32[1,8,256,256]{3,2,1,0:T(8,128)} copy(f32[1,8,256,256]{3,2,1,0:T(8,128)} %get-tuple-element.6) | data formatting | bytes 4194304

commit v2 on v1

--- a/solution.py
+++ b/solution.py
@@ -90,9 +90,9 @@
 def kernel(
     gz, pairs,
     pidx, pweight, orbitals, pot, res_out, en_out,
-    orb0, orb1, orb2, orb3, orb4, orb5, orb6, orb7, px, tmp, f, a, b, g0, g0o, s1, a1, b1, t1, g1, g1o, pe1,
+    orb0, orb1, orb2, orb3, orb4, orb5, orb6, orb7, px, tmp, pidx2, fx, f, a, b, g0, g0o, s1, a1, b1, t1, g1, g1o, pe1,
     s2, a2, b2, t2, pe2, t3, s3, a3, b3, sums, ens, obuf,
-    orb_sem, fs, fr, g0s, g0r, h1s, h1r, g1s, g1r, h2s, h2r, t3s, t3r, ss, sr, es, er, out_sem,
+    orb_sem, ixs, ixr, fs, fr, g0s, g0r, h1s, h1r, g1s, g1r, h2s, h2r, t3s, t3r, ss, sr, es, er, out_sem,
 ):
     d = lax.axis_index("gz")
     me = lax.axis_index("pair")
@@ -120,6 +120,15 @@
     @pl.loop(1, pairs)
     def _(o):
         pl.semaphore_signal(barrier, inc=1, device_id={"pair": lax.rem(me + o, pairs)}, device_id_type=MESH)
+
+    other = lax.rem(me + pairs // 2, pairs)
+    even = lax.rem(d, 2) == 0
+    across = jnp.where(even, d - 1, d + 1)
+    has_across = jnp.logical_and(across >= 0, across < gz)
+
+    @pl.when(has_across)
+    def _():
+        pl.semaphore_signal(barrier, inc=1, device_id={"gz": across, "pair": other}, device_id_type=MESH)
 
     px[...] = selection((256, 256), lambda i, j: j == (i & 1) * 128 + (i >> 1))
     pad0 = jnp.zeros((4, PAD, 128), F32)
@@ -192,19 +201,23 @@
         a3[q] = jnp.zeros((48, 128), F32)
         b3[q] = jnp.zeros((48, 128), F32)
 
-    i0, i1 = pidx[0, 0], pidx[0, 1]
-
-    for i, z in enumerate((0, 7, 1, 6, 2, 5, 3, 4)):
-        orb_copy(z).wait()
-        slot = i % 2
-        left = jnp.dot(orb[z][i0], px[...], preferred_element_type=F32)
-        right = jnp.dot(orb[z][i1], px[...], preferred_element_type=F32)
+    def density(z, which, slot, put):
+        left = jnp.dot(orb[z][which[0, 0]], px[...], preferred_element_type=F32)
+        right = jnp.dot(orb[z][which[0, 1]], px[...], preferred_element_type=F32)
         both = left * right
         tmp[slot, 0] = both[:, :128]
         tmp[slot, 1] = both[:, 128:]
         for yp in range(2):
             for xp in range(2):
-                f[z + 4, 2 * yp + xp, pl.ds(PAD, 128), :] = tmp[slot, xp, pl.ds(yp, 128, stride=2), :]
+                put(2 * yp + xp, tmp[slot, xp, pl.ds(yp, 128, stride=2), :])
+
+    for i, z in enumerate((0, 7, 1, 6, 2, 5, 3, 4)):
+        orb_copy(z).wait()
+
+        def put(ph, value):
+            f[z + 4, ph, pl.ds(PAD, 128), :] = value
+
+        density(z, pidx, i % 2, put)
 
     def w_plane(z, lo, hi):
         for r in range(0, 128, CH):
@@ -221,7 +234,10 @@
     w_plane(4, False, True)
     w_plane(11, True, False)
 
-    pl.semaphore_wait(barrier, gz - 1 + pairs - 1)
+    pl.semaphore_wait(barrier, gz - 1 + pairs - 1 + has_across.astype(jnp.int32))
+
+    index_copy = remote(pidx, pidx2, ixs.at[0], ixr.at[0], pair=other)
+    index_copy.start()
 
     for side, z in ((0, 4), (1, 11)):
         for r in range(0, 128, CH):
@@ -246,29 +262,46 @@
     def _():
         g0_hi.start()
 
-    def f_copy(side, k):
-        if side == 0:
-            return remote(
-                f.at[4 + k, :, pl.ds(PAD, 128), :], f.at[12 + k, :, pl.ds(PAD, 128), :],
-                fs.at[0, k], fr.at[1, k], gz=jnp.maximum(d - 1, 0),
-            )
+    turn = lax.rem(d, 4)
+    straight = jnp.logical_or(turn == 1, turn == 2)
+
+    def f_copy(side, far, of_other):
+        k = far if side == 0 else 3 - far
+        here = k if side == 0 else 4 + k
+        there = 12 + k if side == 0 else k
+        to = jnp.maximum(d - 1, 0) if side == 0 else jnp.minimum(d + 1, gz - 1)
+        landed = f.at[there, :, pl.ds(PAD, 128), :]
+        if of_other:
+            return remote(fx.at[k], landed, fs.at[side, far], fr.at[1 - side, far], gz=to, pair=other)
         return remote(
-            f.at[8 + k, :, pl.ds(PAD, 128), :], f.at[k, :, pl.ds(PAD, 128), :],
-            fs.at[1, k], fr.at[0, k], gz=jnp.minimum(d + 1, gz - 1),
+            f.at[4 + here, :, pl.ds(PAD, 128), :], landed, fs.at[side, far], fr.at[1 - side, far], gz=to, pair=me
         )
 
-    def f_start(*which):
-        @pl.when(has_lo)
-        def _():
-            for k in which:
-                f_copy(0, k).start()
-
-        @pl.when(has_hi)
-        def _():
-            for k in which:
-                f_copy(1, 3 - k).start()
-
-    f_start(0)
+    def on_chip(act):
+        for side, cond in ((0, jnp.logical_not(even)), (1, even)):
+            @pl.when(cond)
+            def _():
+                for far in range(4):
+                    act(side, far, False)
+
+    def crossing(far, act, of_other):
+        for side, cond in ((0, jnp.logical_and(even, has_lo)), (1, jnp.logical_and(jnp.logical_not(even), has_hi))):
+            if far == 3:
+                cond = jnp.logical_and(cond, jnp.logical_not(straight) if of_other else straight)
+            elif not of_other:
+                continue
+
+            @pl.when(cond)
+            def _():
+                act(side, far, of_other)
+
+    def begin(side, far, of_other):
+        f_copy(side, far, of_other).start()
+
+    def sent(side, far, of_other):
+        f_copy(side, far, of_other).wait_send()
+
+    on_chip(begin)
 
     @pl.loop(5, 11)
     def _(z):
@@ -293,6 +326,20 @@
                 q = ((src[0] + src[1]) + (src[2] + src[3])) + N81 * (zs - 4.0 * total + shifts)
                 out = q if out is None else out + q
             s1[5 + j, pl.ds(PAD + r, CH), :] = 0.5 * out
+
+    index_copy.wait_recv()
+    for far in range(4):
+        for side, cond in ((0, even), (1, jnp.logical_not(even))):
+            k = far if side == 0 else 3 - far
+
+            def put_other(ph, value):
+                fx[k, ph] = value
+
+            @pl.when(cond)
+            def _():
+                density(k + 4 * side, pidx2, far % 2, put_other)
+
+        crossing(far, begin, True)
 
     @pl.when(has_lo)
     def _():
@@ -371,8 +418,6 @@
             def _():
                 h1_copy(i).start()
 
-    h1_start()
-
     @pl.when(has_lo)
     def _():
         g1_hi.wait_recv()
@@ -431,7 +476,8 @@
         def _():
             h2_copy(i).start()
 
-    f_start(1, 2, 3)
+    h1_start()
+    crossing(3, begin, False)
 
     @pl.loop(1, gz)
     def _(o):
@@ -541,13 +587,13 @@
 
     @pl.when(has_lo)
     def _():
-        for k in range(4):
-            f_copy(1, k).wait_recv()
+        for far in range(4):
+            f_copy(1, far, False).wait_recv()
 
     @pl.when(has_hi)
     def _():
-        for k in range(4):
-            f_copy(0, k).wait_recv()
+        for far in range(4):
+            f_copy(0, far, False).wait_recv()
 
     lo0, hi0 = bounds(-3, 10, 8)
 
@@ -596,8 +642,7 @@
 
     zero = jnp.zeros((8, 128), F32)
     squares, products = lax.fori_loop(4, 12, final, (zero, zero))
-    sums[d, pl.ds(0, 8), :] = squares
-    sums[d, pl.ds(8, 8), :] = products
+    sums[d] = jnp.concatenate([squares.sum(axis=0, keepdims=True), products.sum(axis=0, keepdims=True)], axis=0)
 
     @pl.loop(1, gz)
     def _(o):
@@ -631,13 +676,13 @@
     for e in range(1, gz):
         total = total + sums[e]
     cells = 1.0 / (gz * 8 * 256 * 256)
-    ens[me] = pweight[0] * total[8:]
+    ens[me] = pweight[0] * total[1:]
 
     @pl.loop(1, pairs)
     def _(o):
         remote(ens.at[me], ens.at[me], es.at[o], er.at[me], pair=lax.rem(me + o, pairs)).start()
 
-    norm = jnp.sqrt(jnp.full((8, 128), jnp.sum(total[:8]) * cells, F32))
+    norm = jnp.sqrt(jnp.full((8, 128), jnp.sum(total[:1]) * cells, F32))
     res_out[0] = jnp.max(norm)
 
     @pl.loop(1, pairs)
@@ -655,8 +700,12 @@
         def _():
             (g0_lo, g0_hi)[side].wait_send()
             (g1_lo, g1_hi)[side].wait_send()
-            for k in range(4):
-                f_copy(side, k).wait_send()
+
+    index_copy.wait_send()
+    on_chip(sent)
+    for far in range(4):
+        crossing(far, sent, True)
+    crossing(3, sent, False)
 
     for i in range(4):
         @pl.when(h1_sends[i])
@@ -711,6 +760,8 @@
                 *[vmem((8, 256, 256), BF16)] * 8,
                 vmem((256, 256), BF16),
                 vmem((2, 2, 256, 128), F32),
+                pltpu.SMEM((1, 2), jnp.int32),
+                vmem((4, 4, 128, 128), F32),
                 field, field, field,
                 vmem((2, 128, 128), F32), vmem((2, 128, 128), F32),
                 level1, level1, level1,
@@ -723,10 +774,11 @@
                 vmem((gz, 32, 128), F32),
                 vmem((4, 32, 128), F32),
                 level3, level3,
-                vmem((gz, 16, 128), F32),
-                vmem((pairs, 8, 128), F32),
+                vmem((gz, 2, 128), F32),
+                vmem((pairs, 1, 128), F32),
                 vmem((8, 2, 256, 128), F32),
                 dma((8,)),
+                dma((1,)), dma((1,)),
                 dma((2, 4)), dma((2, 4)),
                 dma((2,)), dma((2,)),
                 dma((4,)), dma((4,)),

time: 75.9 us -> 66.6 us (0.88)
  Pallas kernels: 67.9 us -> 58.6 us
    pallas_call x1, Pallas kernels: 67.9 us -> 58.6 us  [per_device(): pl.pallas_call(functools.partial(kernel, gz, pairs), out_shape=(jax.Shape...]
where the time goes in v2:
time: 66.6 us; the launch traced here: 66.5 us
  Pallas kernels  58.6 us (88%)
  between operations  4.77 us (7%)
  local copies, waits for them, and re-layouts  3.05 us (5%)
    pallas_call x1, Pallas kernels, per_device(): pl.pallas_call(functools.partial(kernel, gz, pairs), out_shape=(jax.Shape...  58.6 us
    unnamed x1, local copies, waits for them, and re-layouts  3.05 us

profile of v2, /device:TPU:1, one launch (start us, length us, event | category | flops | bytes accessed | tf_op | source)
XLA Modules:
  0.0 66.5 jit_solution(12956994167585856866)
XLA Ops:
  1.3 58.6 %vcycle.1 = (f32[1,8,256,256]{3,2,1,0:T(8,128)}, f32[1]{0:T(128)}, f32[1]{0:T(128)}) custom-call(s32[1,2]{1,0:T(1,128)} %pidx.1, f32[1]{0:T(128)S(6)} %copy.9.pweight, bf16[8,8,256,256]{3,2,1,0:T(8,128)(2,1)} %orbitals.1), custom_call_target="tpu_custom_call" | custom-call | tf_op jit(solution)/shard_map/vcycle/pallas_call | solution.py:742
  59.9 3.0 %copy.10 = f32[1,8,256,256]{3,2,1,0:T(8,128)} copy(f32[1,8,256,256]{3,2,1,0:T(8,128)} %get-tuple-element.6) | data formatting | bytes 4194304

commit v3 on v2

--- a/solution.py
+++ b/solution.py
@@ -89,10 +89,10 @@
 
 def kernel(
     gz, pairs,
-    pidx, pweight, orbitals, pot, res_out, en_out,
-    orb0, orb1, orb2, orb3, orb4, orb5, orb6, orb7, px, tmp, pidx2, fx, f, a, b, g0, g0o, s1, a1, b1, t1, g1, g1o, pe1,
-    s2, a2, b2, t2, pe2, t3, s3, a3, b3, sums, ens, obuf,
-    orb_sem, ixs, ixr, fs, fr, g0s, g0r, h1s, h1r, g1s, g1r, h2s, h2r, t3s, t3r, ss, sr, es, er, out_sem,
+    index_in, weight_in, orbitals, pot, res_out, en_out,
+    orb0, orb1, orb2, orb3, orb4, orb5, orb6, orb7, px, tmp, pidx, pweight, pidx2, fx, f, a, b, g0, g0o, s1, a1, b1, t1, g1, g1o, pe1,
+    s2, a2, b2, t2, pe2, t3, s3, a3, b3, sums, ens,
+    scalar_sem, orb_sem, ixs, ixr, fs, fr, g0s, g0r, h1s, h1r, g1s, g1r, h2s, h2r, t3s, t3r, ss, sr, es, er,
 ):
     d = lax.axis_index("gz")
     me = lax.axis_index("pair")
@@ -109,6 +109,10 @@
     def orb_copy(z):
         return pltpu.make_async_copy(orbitals.at[:, z], orb[z], orb_sem.at[z])
 
+    index_load = pltpu.make_async_copy(index_in, pidx, scalar_sem.at[0])
+    weight_load = pltpu.make_async_copy(weight_in, pweight, scalar_sem.at[1])
+    index_load.start()
+    weight_load.start()
     for z in (0, 7, 1, 6, 2, 5, 3, 4):
         orb_copy(z).start()
     barrier = pltpu.get_barrier_semaphore()
@@ -211,6 +215,8 @@
             for xp in range(2):
                 put(2 * yp + xp, tmp[slot, xp, pl.ds(yp, 128, stride=2), :])
 
+    index_load.wait()
+    weight_load.wait()
     for i, z in enumerate((0, 7, 1, 6, 2, 5, 3, 4)):
         orb_copy(z).wait()
 
@@ -286,7 +292,7 @@
 
     def crossing(far, act, of_other):
         for side, cond in ((0, jnp.logical_and(even, has_lo)), (1, jnp.logical_and(jnp.logical_not(even), has_hi))):
-            if far == 3:
+            if far in (0, 3):
                 cond = jnp.logical_and(cond, jnp.logical_not(straight) if of_other else straight)
             elif not of_other:
                 continue
@@ -301,6 +307,7 @@
     def sent(side, far, of_other):
         f_copy(side, far, of_other).wait_send()
 
+    crossing(0, begin, False)
     on_chip(begin)
 
     @pl.loop(5, 11)
@@ -326,11 +333,86 @@
                 q = ((src[0] + src[1]) + (src[2] + src[3])) + N81 * (zs - 4.0 * total + shifts)
                 out = q if out is None else out + q
             s1[5 + j, pl.ds(PAD + r, CH), :] = 0.5 * out
+            b1[5 + j, pl.ds(PAD + r, CH), :] = 0.5 * out
+
+    def ypair(ref, slot, n):
+        return ref[slot, pl.ds(0, n, stride=2), :] + ref[slot, pl.ds(1, n, stride=2), :]
+
+    def inside(step):
+        at = d + step
+        return jnp.logical_and(at >= 0, at < gz)
+
+    flag2 = {p: inside(p - 3).astype(F32) for p in range(1, 6)}
+    m_first = selection((128, 128), lambda i, j: (i >> 1) == j)
+    m_second = selection((128, 128), lambda i, j: (i >> 1) + 64 == j)
+    low_half = lane_iota((64, 128)) < 64
+
+    def nb2(ref, p, c):
+        z = roll(c + jnp.where(low_half, crow(ref, p + 1, 0, 64), crow(ref, p - 1, 0, 64)), 64)
+        return nbxy(ref, p, 0, 64, c, 64) + z
+
+    b1[4, pl.ds(PAD, 128), :] = flo * g0o[0]
+    b1[9, pl.ds(PAD, 128), :] = fhi * g0o[1]
+
+    @pl.loop(3, 11)
+    def _(z):
+        flag = jnp.where(z < 5, flo, jnp.where(z > 8, fhi, 1.0))
+        for r in range(0, 128, 64):
+            c = crow(b1, z, r, 64)
+            nb = nbxy(b1, z, r, 64, c, 128) + (crow(b1, z - 1, r, 64) + crow(b1, z + 1, r, 64))
+            a1[z, pl.ds(PAD + r, 64), :] = flag * (12.0 * c + nb)
+
+    @pl.loop(0, 6)
+    def _(j):
+        for r in range(0, 128, 64):
+            out = None
+            for dz in range(2):
+                z = 1 + 2 * j + dz
+                c = crow(a1, z, r, 64)
+                nb = nbxy(a1, z, r, 64, c, 128) + (crow(a1, z - 1, r, 64) + crow(a1, z + 1, r, 64))
+                q = crow(b1, z, r, 64) + N81 * (nb - 6.0 * c)
+                out = q if out is None else out + q
+            t1[j, pl.ds(r, 64), :] = 0.5 * out
+
+    for p in range(3):
+        b2[2 + p, pl.ds(PAD, 64), :] = flag2[2 + p] * (
+            split_dot(ypair(t1, 2 * p, 64), m_first) + split_dot(ypair(t1, 2 * p + 1, 64), m_second)
+        )
+    for p in range(1, 6):
+        c = crow(b2, p, 0, 64)
+        a2[p, pl.ds(PAD, 64), :] = flag2[p] * (12.0 * c + nb2(b2, p, c))
+    for p in range(1, 6):
+        w = crow(a2, p, 0, 64)
+        t2[p - 1] = crow(b2, p, 0, 64) + N81 * (nb2(a2, p, w) - 6.0 * w)
+    tile = None
+    for p in range(1, 5):
+        block = lax.rem(d + p - 2 + gz, 4) * 32
+        m = selection((128, 128), lambda i, j: ((i & 63) >> 1) + block == j)
+        part = split_dot(ypair(t2, p, 32), m)
+        tile = part if tile is None else tile + part
+    t3[d, pl.ds(0, 32), :] = 0.5 * tile
+    m = selection((128, 128), lambda i, j: ((i & 63) >> 1) == (j & 31))
+    part = split_dot(ypair(t2, 0, 32), m)
+    block8 = lane_iota((8, 128)) // 32
+    row = part[0:8]
+    for k in range(1, 4):
+        row = jnp.where(block8 == k, part[8 * k:8 * k + 8], row)
+    t3[d, pl.ds(32, 8), :] = 0.5 * row
+
+    def t3_copy(o):
+        to = lax.rem(d + o, gz)
+        return remote(t3.at[d], t3.at[d], t3s.at[o], t3r.at[d], gz=to)
+
+    @pl.loop(1, gz)
+    def _(o):
+        t3_copy(o).start()
 
     index_copy.wait_recv()
     for far in range(4):
         for side, cond in ((0, even), (1, jnp.logical_not(even))):
             k = far if side == 0 else 3 - far
+            if far in (0, 3):
+                cond = jnp.logical_and(cond, jnp.logical_not(straight))
 
             def put_other(ph, value):
                 fx[k, ph] = value
@@ -381,11 +463,6 @@
                 out = q if out is None else out + q
             t1[slot, pl.ds(r, 64), :] = 0.5 * out
 
-    def ypair(ref, slot, n):
-        return ref[slot, pl.ds(0, n, stride=2), :] + ref[slot, pl.ds(1, n, stride=2), :]
-
-    m_first = selection((128, 128), lambda i, j: (i >> 1) == j)
-    m_second = selection((128, 128), lambda i, j: (i >> 1) + 64 == j)
     g1o[0] = split_dot(ypair(t1, 0, 64), m_second)
     g1o[1] = split_dot(ypair(t1, 3, 64), m_first)
     g1_lo, g1_hi = exchange(g1o, g1, g1s, g1r)
@@ -418,6 +495,8 @@
             def _():
                 h1_copy(i).start()
 
+    h1_start()
+
     @pl.when(has_lo)
     def _():
         g1_hi.wait_recv()
@@ -427,12 +506,6 @@
     def _():
         g1_lo.wait_recv()
         s2[3, pl.ds(PAD, 64), :] += g1[1]
-
-    low_half = lane_iota((64, 128)) < 64
-
-    def nb2(ref, p, c):
-        z = roll(c + jnp.where(low_half, crow(ref, p + 1, 0, 64), crow(ref, p - 1, 0, 64)), 64)
-        return nbxy(ref, p, 0, 64, c, 64) + z
 
     def h2_copy(i):
         step = (-3, -2, -1, 1, 2, 3)[i]
@@ -441,42 +514,11 @@
             s2.at[3, pl.ds(PAD, 64), :], s2.at[3 - step, pl.ds(PAD, 64), :], h2s.at[i], h2r.at[i], gz=to
         )
 
-    def inside(step):
-        at = d + step
-        return jnp.logical_and(at >= 0, at < gz)
-
-    c = crow(s2, 3, 0, 64)
-    turned = roll(c, 64)
-    w0 = 12.0 * c + nbxy(s2, 3, 0, 64, c, 64) + turned
-    a2[3, pl.ds(PAD, 64), :] = w0
-    a2[2, pl.ds(PAD, 64), :] = flo * jnp.where(low_half, 0.0, turned)
-    a2[4, pl.ds(PAD, 64), :] = fhi * jnp.where(low_half, turned, 0.0)
-    for p in (2, 3, 4):
-        w = crow(a2, p, 0, 64)
-        r = N81 * (nb2(a2, p, w) - 6.0 * w)
-        t2[p - 2] = r + c if p == 3 else r
-    tile = None
-    for p in range(3):
-        block = lax.rem(d + p - 1 + gz, 4) * 32
-        m = selection((128, 128), lambda i, j: ((i & 63) >> 1) + block == j)
-        part = split_dot(ypair(t2, p, 32), m)
-        tile = part if tile is None else tile + part
-    t3[d] = 0.5 * tile
-
-    def t3_copy(o):
-        to = lax.rem(d + o, gz)
-        return remote(t3.at[d], t3.at[d], t3s.at[o], t3r.at[d], gz=to)
-
-    @pl.loop(1, gz)
-    def _(o):
-        t3_copy(o).start()
-
     for i, step in enumerate((-3, -2, -1, 1, 2, 3)):
         @pl.when(inside(step))
         def _():
             h2_copy(i).start()
 
-    h1_start()
     crossing(3, begin, False)
 
     @pl.loop(1, gz)
@@ -487,17 +529,21 @@
     lane32 = lane_iota((32, 128))
     for q in range(4):
         total = None
-        for e in range(max(4 * q - 1, 0), min(4 * q + 5, gz)):
-            x = t3[e]
-            if e == 4 * q - 1:
-                x = jnp.where(lane32 < 32, x, 0.0)
-            elif e == 4 * q + 4:
-                x = jnp.where(lane32 >= 96, x, 0.0)
-            elif e == 4 * q:
-                x = jnp.where(lane32 < 96, x, 0.0)
-            elif e == 4 * q + 3:
-                x = jnp.where(lane32 >= 32, x, 0.0)
-            total = x if total is None else total + x
+        for e in range(max(4 * q - 2, 0), min(4 * q + 6, gz)):
+            low, high = max(e - 1 - 4 * q, 0), min(e + 2 - 4 * q, 3)
+            parts = []
+            if low <= high:
+                x = t3[e, pl.ds(0, 32), :]
+                if (low, high) != (0, 3):
+                    x = jnp.where(jnp.logical_and(lane32 >= 32 * low, lane32 < 32 * high + 32), x, 0.0)
+                parts.append(x)
+            block = e - 2 - 4 * q
+            if 0 <= block < 4:
+                x = t3[e, pl.ds(32, 8), :]
+                pieces = [jnp.where(block8 == block, roll(x, 32 * (block - k)), 0.0) for k in range(4)]
+                parts.append(jnp.concatenate(pieces, axis=0))
+            for x in parts:
+                total = x if total is None else total + x
         s3[q] = total * NINTH
         a3[q, pl.ds(PAD, 32), :] = total * NINTH
 
@@ -523,7 +569,6 @@
         def _():
             h2_copy(i).wait_recv()
 
-    flag2 = {p: inside(p - 3).astype(F32) for p in range(1, 6)}
     for p in range(1, 6):
         at = d + p - 3
         q = jnp.clip(at // 4, 0, 3)
@@ -650,11 +695,6 @@
 
     px[...] = selection((256, 256), lambda i, j: i == (j & 1) * 128 + (j >> 1))
 
-    def out_copy(z, half):
-        return pltpu.make_async_copy(
-            obuf.at[z, half], pot.at[0, z, :, pl.ds(128 * half, 128)], out_sem.at[z, half]
-        )
-
     @pl.loop(0, 8)
     def _(z):
         for yp in range(2):
@@ -663,9 +703,9 @@
             )
             y = split_dot(x, px[...])
             for half in range(2):
-                obuf[z, half, pl.ds(yp, 128, stride=2), :] = y[:, 128 * half:128 * half + 128]
+                tmp[z % 2, half, pl.ds(yp, 128, stride=2), :] = y[:, 128 * half:128 * half + 128]
         for half in range(2):
-            out_copy(z, half).start()
+            pot[0, z, :, pl.ds(128 * half, 128)] = tmp[z % 2, half]
 
     @pl.loop(1, gz)
     def _(o):
@@ -682,8 +722,7 @@
     def _(o):
         remote(ens.at[me], ens.at[me], es.at[o], er.at[me], pair=lax.rem(me + o, pairs)).start()
 
-    norm = jnp.sqrt(jnp.full((8, 128), jnp.sum(total[:1]) * cells, F32))
-    res_out[0] = jnp.max(norm)
+    res_out[...] = jnp.sqrt(jnp.sum(total[:1], axis=1, keepdims=True) * cells)
 
     @pl.loop(1, pairs)
     def _(o):
@@ -693,7 +732,7 @@
     energy = ens[0]
     for e in range(1, pairs):
         energy = energy + ens[e]
-    en_out[0] = jnp.sum(energy) * (-0.5 * cells)
+    en_out[...] = jnp.sum(energy, axis=1, keepdims=True) * (-0.5 * cells)
 
     for cond, side in ((has_lo, 0), (has_hi, 1)):
         @pl.when(cond)
@@ -705,6 +744,7 @@
     on_chip(sent)
     for far in range(4):
         crossing(far, sent, True)
+    crossing(0, sent, False)
     crossing(3, sent, False)
 
     for i in range(4):
@@ -725,11 +765,6 @@
     @pl.loop(1, pairs)
     def _(o):
         remote(ens.at[me], ens.at[me], es.at[o], er.at[me], pair=lax.rem(me + o, pairs)).wait_send()
-
-    @pl.loop(0, 8)
-    def _(z):
-        for half in range(2):
-            out_copy(z, half).wait()
 
 
 def solution(mesh):
@@ -739,44 +774,46 @@
     level1, level2, level3 = vmem((14, 144, 128), F32), vmem((7, 80, 128), F32), vmem((4, 48, 128), F32)
 
     def per_device(orbitals, pair_index, pair_weight):
-        return pl.pallas_call(
+        potential, norm, energy = pl.pallas_call(
             functools.partial(kernel, gz, pairs),
             out_shape=(
                 jax.ShapeDtypeStruct((1, 8, 256, 256), F32),
-                jax.ShapeDtypeStruct((1,), F32),
-                jax.ShapeDtypeStruct((1,), F32),
+                jax.ShapeDtypeStruct((1, 1), F32),
+                jax.ShapeDtypeStruct((1, 1), F32),
             ),
             in_specs=[
-                pl.BlockSpec(memory_space=pltpu.SMEM),
-                pl.BlockSpec(memory_space=pltpu.SMEM),
+                pl.BlockSpec(memory_space=pltpu.HBM),
+                pl.BlockSpec(memory_space=pltpu.HBM),
                 pl.BlockSpec(memory_space=pl.ANY),
             ],
             out_specs=(
-                pl.BlockSpec(memory_space=pl.ANY),
-                pl.BlockSpec(memory_space=pltpu.SMEM),
-                pl.BlockSpec(memory_space=pltpu.SMEM),
+                pl.BlockSpec(memory_space=pltpu.VMEM),
+                pl.BlockSpec(memory_space=pltpu.VMEM),
+                pl.BlockSpec(memory_space=pltpu.VMEM),
             ),
             scratch_shapes=[
                 *[vmem((8, 256, 256), BF16)] * 8,
                 vmem((256, 256), BF16),
                 vmem((2, 2, 256, 128), F32),
                 pltpu.SMEM((1, 2), jnp.int32),
+                pltpu.SMEM((1,), F32),
+                pltpu.SMEM((1, 2), jnp.int32),
                 vmem((4, 4, 128, 128), F32),
                 field, field, field,
                 vmem((2, 128, 128), F32), vmem((2, 128, 128), F32),
                 level1, level1, level1,
-                vmem((4, 128, 128), F32),
+                vmem((6, 128, 128), F32),
                 vmem((2, 64, 128), F32), vmem((2, 64, 128), F32),
                 vmem((6, 128, 128), F32),
                 level2, level2, level2,
-                vmem((3, 64, 128), F32),
                 vmem((5, 64, 128), F32),
-                vmem((gz, 32, 128), F32),
+                vmem((5, 64, 128), F32),
+                vmem((gz, 40, 128), F32),
                 vmem((4, 32, 128), F32),
                 level3, level3,
                 vmem((gz, 2, 128), F32),
                 vmem((pairs, 1, 128), F32),
-                vmem((8, 2, 256, 128), F32),
+                dma((2,)),
                 dma((8,)),
                 dma((1,)), dma((1,)),
                 dma((2, 4)), dma((2, 4)),
@@ -787,13 +824,13 @@
                 dma((gz,)), dma((gz,)),
                 dma((gz,)), dma((gz,)),
                 dma((pairs,)), dma((pairs,)),
-                dma((8, 2)),
             ],
             compiler_params=pltpu.CompilerParams(
-                collective_id=0, has_side_effects=True, vmem_limit_bytes=60 * 1024 * 1024
+                collective_id=0, has_side_effects=True, vmem_limit_bytes=48 * 1024 * 1024
             ),
             name="vcycle",
         )(pair_index, pair_weight, orbitals)
+        return potential, norm.reshape(1), energy.reshape(1)
 
     return jax.shard_map(
         per_device,

time: 66.6 us -> 65 us (0.976)
  local copies, waits for them, and re-layouts: 3.05 us -> 1.97 us
    unnamed x1 -> x3, local copies, waits for them, and re-layouts: 3.05 us -> 1.97 us
where the time goes in v3:
time: 65 us; the launch traced here: 64.8 us
  Pallas kernels  58.1 us (89%)
  between operations  4.82 us (7%)
  local copies, waits for them, and re-layouts  1.97 us (3%)
    pallas_call x1, Pallas kernels, per_device(): pl.pallas_call(functools.partial(kernel, gz, pairs), out_shape=(jax.Shape...  58.1 us
    unnamed x3, local copies, waits for them, and re-layouts  1.97 us

profile of v3, /device:TPU:1, one launch (start us, length us, event | category | flops | bytes accessed | tf_op | source)
XLA Modules:
  0.0 64.8 jit_solution(7061466308170461016)
XLA Ops:
  1.3 0.0 copy-start
  1.3 0.6 copy-done
  1.9 58.1 %vcycle.1 = (f32[1,8,256,256]{3,2,1,0:T(8,128)S(1)}, f32[1,1]{1,0:T(1,128)}, f32[1,1]{1,0:T(1,128)}) custom-call(s32[1,2]{1,0:T(1,128)S(1)} %copy-done, f32[1]{0:T(128)S(6)} %copy.9.weight_in, bf16[8,8,256,256]{3,2,1,0:T(8,128)(2,1)} %orbitals.1), custom_call_target="tpu_custom_call" | custom-call | tf_op jit(solution)/shard_map/vcycle/pallas_call | solution.py:777
  60.0 1.3 %copy.10 = f32[1,8,256,256]{3,2,1,0:T(8,128)} copy(f32[1,8,256,256]{3,2,1,0:T(8,128)S(1)} %get-tuple-element.12) | data formatting | bytes 4194304
Async XLA Ops:
  1.3 0.7 %copy-start = (s32[1,2]{1,0:T(1,128)S(1)}, s32[1,2]{1,0:T(1,128)}, u32[]{:S(2)}) copy-start(s32[1,2]{1,0:T(1,128)} %index_in.1) | copy-start | bytes 28

commit v4 on v3

--- a/solution.py
+++ b/solution.py
@@ -10,6 +10,7 @@
 MESH = pl.DeviceIdType.MESH
 F32, BF16 = jnp.float32, jnp.bfloat16
 PAD = 8
+EARLY = 0
 CH = 32
 NINTH = 1.0 / 9.0
 N81 = 1.0 / 81.0
@@ -90,9 +91,9 @@
 def kernel(
     gz, pairs,
     index_in, weight_in, orbitals, pot, res_out, en_out,
-    orb0, orb1, orb2, orb3, orb4, orb5, orb6, orb7, px, tmp, pidx, pweight, pidx2, fx, f, a, b, g0, g0o, s1, a1, b1, t1, g1, g1o, pe1,
+    orb0, orb1, orb2, orb3, orb4, orb5, orb6, orb7, px, mats, tmp, pidx, pweight, pidx2, fx, f, a, b, g0, g0o, s1, a1, b1, t1, g1, g1o, pe1, e1, e1h,
     s2, a2, b2, t2, pe2, t3, s3, a3, b3, sums, ens,
-    scalar_sem, orb_sem, ixs, ixr, fs, fr, g0s, g0r, h1s, h1r, g1s, g1r, h2s, h2r, t3s, t3r, ss, sr, es, er,
+    scalar_sem, orb_sem, ixs, ixr, fs, fr, g0s, g0r, h1s, h1r, g1s, g1r, e1s, e1r, h2s, h2r, t3s, t3r, ss, sr, es, er,
 ):
     d = lax.axis_index("gz")
     me = lax.axis_index("pair")
@@ -136,6 +137,16 @@
 
     px[...] = selection((256, 256), lambda i, j: j == (i & 1) * 128 + (i >> 1))
     pad0 = jnp.zeros((4, PAD, 128), F32)
+    square = (128, 128)
+    mats[0] = selection(square, lambda i, j: (i >> 1) == j)
+    mats[1] = selection(square, lambda i, j: (i >> 1) + 64 == j)
+    for half in range(2):
+        mats[2 + half] = selection(square, lambda i, j: i == (j >> 1) + 64 * half)
+    for p in range(5):
+        block = lax.rem(d + p - 2 + gz, 4) * 32
+        mats[4 + p] = selection(square, lambda i, j: ((i & 63) >> 1) + block == j)
+        mats[9 + p] = selection(square, lambda i, j: i == ((j & 63) >> 1) + block)
+    mats[14] = selection(square, lambda i, j: ((i & 63) >> 1) == (j & 31))
 
     @pl.loop(0, 16)
     def _(z):
@@ -173,14 +184,6 @@
         clear_outside(12)
         g0[1] = jnp.zeros((128, 128), F32)
         g1[1] = jnp.zeros((64, 128), F32)
-
-    @pl.when(d == 1)
-    def _():
-        s1[0, pl.ds(PAD, 128), :] = jnp.zeros((128, 128), F32)
-
-    @pl.when(d == gz - 2)
-    def _():
-        s1[13, pl.ds(PAD, 128), :] = jnp.zeros((128, 128), F32)
 
     @pl.loop(0, 14)
     def _(z):
@@ -197,7 +200,7 @@
         b2[p] = jnp.zeros((80, 128), F32)
         at = d + p - 3
 
-        @pl.when(jnp.logical_or(at < 0, at >= gz))
+        @pl.when(jnp.logical_or(jnp.logical_or(at < 0, at >= gz), jnp.logical_or(p == 0, p == 6)))
         def _():
             s2[p, pl.ds(PAD, 64), :] = jnp.zeros((64, 128), F32)
 
@@ -270,6 +273,7 @@
 
     turn = lax.rem(d, 4)
     straight = jnp.logical_or(turn == 1, turn == 2)
+    diagonal = jnp.logical_not(straight)
 
     def f_copy(side, far, of_other):
         k = far if side == 0 else 3 - far
@@ -290,10 +294,11 @@
                 for far in range(4):
                     act(side, far, False)
 
-    def crossing(far, act, of_other):
+    def crossing(far, act, of_other, only=True):
         for side, cond in ((0, jnp.logical_and(even, has_lo)), (1, jnp.logical_and(jnp.logical_not(even), has_hi))):
-            if far in (0, 3):
-                cond = jnp.logical_and(cond, jnp.logical_not(straight) if of_other else straight)
+            cond = jnp.logical_and(cond, only)
+            if far == 0:
+                cond = jnp.logical_and(cond, straight if of_other else diagonal)
             elif not of_other:
                 continue
 
@@ -343,8 +348,7 @@
         return jnp.logical_and(at >= 0, at < gz)
 
     flag2 = {p: inside(p - 3).astype(F32) for p in range(1, 6)}
-    m_first = selection((128, 128), lambda i, j: (i >> 1) == j)
-    m_second = selection((128, 128), lambda i, j: (i >> 1) + 64 == j)
+    m_first, m_second = mats[0], mats[1]
     low_half = lane_iota((64, 128)) < 64
 
     def nb2(ref, p, c):
@@ -354,7 +358,7 @@
     b1[4, pl.ds(PAD, 128), :] = flo * g0o[0]
     b1[9, pl.ds(PAD, 128), :] = fhi * g0o[1]
 
-    @pl.loop(3, 11)
+    @pl.loop(3, 11, unroll=4)
     def _(z):
         flag = jnp.where(z < 5, flo, jnp.where(z > 8, fhi, 1.0))
         for r in range(0, 128, 64):
@@ -362,7 +366,7 @@
             nb = nbxy(b1, z, r, 64, c, 128) + (crow(b1, z - 1, r, 64) + crow(b1, z + 1, r, 64))
             a1[z, pl.ds(PAD + r, 64), :] = flag * (12.0 * c + nb)
 
-    @pl.loop(0, 6)
+    @pl.loop(0, 6, unroll=2)
     def _(j):
         for r in range(0, 128, 64):
             out = None
@@ -386,13 +390,10 @@
         t2[p - 1] = crow(b2, p, 0, 64) + N81 * (nb2(a2, p, w) - 6.0 * w)
     tile = None
     for p in range(1, 5):
-        block = lax.rem(d + p - 2 + gz, 4) * 32
-        m = selection((128, 128), lambda i, j: ((i & 63) >> 1) + block == j)
-        part = split_dot(ypair(t2, p, 32), m)
+        part = split_dot(ypair(t2, p, 32), mats[4 + p])
         tile = part if tile is None else tile + part
     t3[d, pl.ds(0, 32), :] = 0.5 * tile
-    m = selection((128, 128), lambda i, j: ((i & 63) >> 1) == (j & 31))
-    part = split_dot(ypair(t2, 0, 32), m)
+    part = split_dot(ypair(t2, 0, 32), mats[14])
     block8 = lane_iota((8, 128)) // 32
     row = part[0:8]
     for k in range(1, 4):
@@ -411,8 +412,8 @@
     for far in range(4):
         for side, cond in ((0, even), (1, jnp.logical_not(even))):
             k = far if side == 0 else 3 - far
-            if far in (0, 3):
-                cond = jnp.logical_and(cond, jnp.logical_not(straight))
+            if far == 0:
+                cond = jnp.logical_and(cond, straight)
 
             def put_other(ph, value):
                 fx[k, ph] = value
@@ -421,7 +422,7 @@
             def _():
                 density(k + 4 * side, pidx2, far % 2, put_other)
 
-        crossing(far, begin, True)
+        crossing(far, begin, True, straight if far > EARLY else True)
 
     @pl.when(has_lo)
     def _():
@@ -478,19 +479,17 @@
     s2[3, pl.ds(PAD, 64), :] = split_dot(ypair(t1, 1, 64), m_first) + split_dot(ypair(t1, 2, 64), m_second)
 
     def h1_copy(i):
-        here, there, step = ((5, 9, -1), (5, 1, 1), (5, 13, -2), (8, 0, 2))[i]
-        n = 4 if abs(step) == 1 else 1
+        here, there, step = ((5, 9, -1), (6, 2, 1))[i]
         to = jnp.clip(d + step, 0, gz - 1)
         return remote(
-            s1.at[pl.ds(here, n), pl.ds(PAD, 128), :], s1.at[pl.ds(there, n), pl.ds(PAD, 128), :],
+            s1.at[pl.ds(here, 3), pl.ds(PAD, 128), :], s1.at[pl.ds(there, 3), pl.ds(PAD, 128), :],
             h1s.at[i], h1r.at[i], gz=to,
         )
 
-    h1_sends = [d >= 1, d <= gz - 2, d >= 2, d <= gz - 3]
-    h1_recvs = [d <= gz - 2, d >= 1, d <= gz - 3, d >= 2]
+    h1_sends, h1_recvs = [has_lo, has_hi], [has_hi, has_lo]
 
     def h1_start():
-        for i in range(4):
+        for i in range(2):
             @pl.when(h1_sends[i])
             def _():
                 h1_copy(i).start()
@@ -508,23 +507,25 @@
         s2[3, pl.ds(PAD, 64), :] += g1[1]
 
     def h2_copy(i):
-        step = (-3, -2, -1, 1, 2, 3)[i]
+        step = (-2, -1, 1, 2)[i]
         to = jnp.clip(d + step, 0, gz - 1)
         return remote(
             s2.at[3, pl.ds(PAD, 64), :], s2.at[3 - step, pl.ds(PAD, 64), :], h2s.at[i], h2r.at[i], gz=to
         )
 
-    for i, step in enumerate((-3, -2, -1, 1, 2, 3)):
+    for i, step in enumerate((-2, -1, 1, 2)):
         @pl.when(inside(step))
         def _():
             h2_copy(i).start()
 
-    crossing(3, begin, False)
 
     @pl.loop(1, gz)
     def _(o):
         peer = lax.rem(d + o, gz)
         remote(t3.at[peer], t3.at[peer], t3s.at[o], t3r.at[peer], gz=peer).wait_recv()
+
+    for far in range(EARLY + 1, 4):
+        crossing(far, begin, True, diagonal)
 
     lane32 = lane_iota((32, 128))
     for q in range(4):
@@ -564,7 +565,7 @@
 
     sweep3(a3, b3)
 
-    for i, step in enumerate((-3, -2, -1, 1, 2, 3)):
+    for i, step in enumerate((-2, -1, 1, 2)):
         @pl.when(inside(-step))
         def _():
             h2_copy(i).wait_recv()
@@ -572,9 +573,7 @@
     for p in range(1, 6):
         at = d + p - 3
         q = jnp.clip(at // 4, 0, 3)
-        block = lax.rem(at + gz, 4) * 32
-        m = selection((128, 128), lambda i, j: i == ((j & 63) >> 1) + block)
-        e = split_dot(b3[q, pl.ds(PAD, 32), :], m)
+        e = split_dot(b3[q, pl.ds(PAD, 32), :], mats[8 + p])
         pe2[p - 1, pl.ds(0, 32, stride=2), :] = e
         pe2[p - 1, pl.ds(1, 32, stride=2), :] = e
     for p in range(1, 6):
@@ -588,78 +587,83 @@
             (1.0 / 3.0) * c + NINTH * (nb2(src, p, c) + crow(s2, p, 0, 64))
         )
 
-    for p in range(1, 6):
+    for p in range(2, 5):
         sweep2(a2, b2, p)
     for p in range(2, 5):
         sweep2(b2, a2, p)
 
-    for i in range(4):
+    for i in range(2):
         @pl.when(h1_recvs[i])
         def _():
             h1_copy(i).wait_recv()
 
-    for half in range(2):
-        m = selection((128, 128), lambda i, j: i == (j >> 1) + 64 * half)
-        for p in range(3):
-            e = split_dot(a2[2 + p, pl.ds(PAD, 64), :], m)
-            pe1[2 * p + half, pl.ds(0, 64, stride=2), :] = e
-            pe1[2 * p + half, pl.ds(1, 64, stride=2), :] = e
-
-    def bounds(first, last, own):
-        return jnp.where(has_lo, first, 0), jnp.where(has_hi, last + 1, own)
-
-    lo1, hi1 = bounds(-4, 7, 4)
-
-    @pl.loop(lo1 + 5, hi1 + 5)
-    def _(z):
+    for j in range(1, 5):
+        e = split_dot(a2[2 + j // 2, pl.ds(PAD, 64), :], mats[2 + j % 2])
+        pe1[j, pl.ds(0, 64, stride=2), :] = e
+        pe1[j, pl.ds(1, 64, stride=2), :] = e
+
+    def in_grid(z):
+        return jnp.where(z < 5, flo, jnp.where(z > 8, fhi, 1.0))
+
+    def nb1(ref, z, r, c):
+        return nbxy(ref, z, r, 64, c, 128) + (crow(ref, z - 1, r, 64) + crow(ref, z + 1, r, 64))
+
+    @pl.loop(3, 11, unroll=4)
+    def _(z):
+        flag = in_grid(z)
         for r in range(0, 128, 64):
             c = crow(s1, z, r, 64)
-            w = 12.0 * c + nbxy(s1, z, r, 64, c, 128) + (crow(s1, z - 1, r, 64) + crow(s1, z + 1, r, 64))
-            a1[z, pl.ds(PAD + r, 64), :] = N81 * w + pe1[(z - 1) // 2, pl.ds(r, 64), :]
-
-    def sweep1(src, dst, first, last):
-        lo, hi = bounds(first, last, 4)
-
-        @pl.loop(lo + 5, hi + 5)
-        def _(z):
-            for r in range(0, 128, 64):
-                c = crow(src, z, r, 64)
-                nb = nbxy(src, z, r, 64, c, 128) + (crow(src, z - 1, r, 64) + crow(src, z + 1, r, 64))
-                dst[z, pl.ds(PAD + r, 64), :] = (1.0 / 3.0) * c + NINTH * (nb + crow(s1, z, r, 64))
-
-    sweep1(a1, b1, -3, 6)
-    sweep1(b1, a1, -2, 5)
+            w = 12.0 * c + nb1(s1, z, r, c)
+            a1[z, pl.ds(PAD + r, 64), :] = flag * (N81 * w + pe1[(z - 1) // 2, pl.ds(r, 64), :])
+
+    @pl.loop(4, 10, unroll=3)
+    def _(z):
+        flag = in_grid(z)
+        for r in range(0, 128, 64):
+            c = crow(a1, z, r, 64)
+            t = nb1(a1, z, r, c) + crow(s1, z, r, 64)
+            b1[z, pl.ds(PAD + r, 64), :] = flag * ((1.0 / 3.0) * c + NINTH * t)
+
+    @pl.loop(5, 9, unroll=4)
+    def _(z):
+        for r in range(0, 128, 64):
+            c = crow(b1, z, r, 64)
+            t = nb1(b1, z, r, c) + crow(s1, z, r, 64)
+            e1[z - 5, pl.ds(r, 64), :] = (1.0 / 3.0) * c + NINTH * t
+
+    e1_lo = remote(
+        e1.at[pl.ds(0, 2)], e1h.at[1], e1s.at[0], e1r.at[1], gz=jnp.maximum(d - 1, 0)
+    )
+    e1_hi = remote(
+        e1.at[pl.ds(2, 2)], e1h.at[0], e1s.at[1], e1r.at[0], gz=jnp.minimum(d + 1, gz - 1)
+    )
 
     @pl.when(has_lo)
     def _():
-        for far in range(4):
-            f_copy(1, far, False).wait_recv()
+        e1_lo.start()
 
     @pl.when(has_hi)
     def _():
-        for far in range(4):
-            f_copy(0, far, False).wait_recv()
-
-    lo0, hi0 = bounds(-3, 10, 8)
-
-    @pl.loop(lo0 + 4, 5)
-    def _(z):
-        w_plane(z, True, True)
-
-    @pl.loop(11, hi0 + 4)
-    def _(z):
-        w_plane(z, True, True)
-
-    @pl.loop(lo0 + 4, hi0 + 4)
-    def _(z):
-        e = a1[z // 2 + 3, pl.ds(PAD, 128), :]
+        e1_hi.start()
+
+    def f_wait(*which):
+        @pl.when(has_lo)
+        def _():
+            for far in which:
+                f_copy(1, far, False).wait_recv()
+
+        @pl.when(has_hi)
+        def _():
+            for far in which:
+                f_copy(0, far, False).wait_recv()
+
+    def correct(z, ref, k):
+        e = ref[k]
         for ph in range(4):
             a[z, ph, pl.ds(PAD, 128), :] = N81 * a[z, ph, pl.ds(PAD, 128), :] + e
 
     def sweep0(src, dst, first, last):
-        lo, hi = bounds(first, last, 8)
-
-        @pl.loop(lo + 4, hi + 4)
+        @pl.loop(first + 4, last + 5)
         def _(z):
             for r in range(0, 128, CH):
                 c = center(src, z, r, CH)
@@ -669,8 +673,49 @@
                     t = t + rows(f, z, ph, r, CH)
                     dst[z, ph, pl.ds(PAD + r, CH), :] = (1.0 / 3.0) * c[ph] + NINTH * t
 
-    sweep0(a, b, -2, 9)
-    sweep0(b, a, -1, 8)
+    def below(first):
+        return jnp.where(has_lo, first, 0)
+
+    def above(last):
+        return jnp.where(has_hi, last, 7)
+
+    f_wait(0)
+    w_plane(4, True, True)
+    w_plane(11, True, True)
+
+    @pl.loop(0, 8)
+    def _(z):
+        correct(z + 4, e1, z // 2)
+
+    sweep0(a, b, 1, 6)
+    sweep0(b, a, 2, 5)
+
+    f_wait(1, 2, 3)
+
+    @pl.loop(below(-3) + 4, 4)
+    def _(z):
+        w_plane(z, True, True)
+
+    @pl.loop(12, above(10) + 5)
+    def _(z):
+        w_plane(z, True, True)
+
+    @pl.when(has_lo)
+    def _():
+        e1_hi.wait_recv()
+        for z in range(-3, 0):
+            correct(z + 4, e1h.at[0], (z + 4) // 2)
+
+    @pl.when(has_hi)
+    def _():
+        e1_lo.wait_recv()
+        for z in range(8, 11):
+            correct(z + 4, e1h.at[1], (z - 8) // 2)
+
+    sweep0(a, b, below(-2), 0)
+    sweep0(a, b, 7, above(9))
+    sweep0(b, a, below(-1), 1)
+    sweep0(b, a, 6, above(8))
 
     def final(z, carry):
         squares, products = carry
@@ -716,7 +761,7 @@
     for e in range(1, gz):
         total = total + sums[e]
     cells = 1.0 / (gz * 8 * 256 * 256)
-    ens[me] = pweight[0] * total[1:]
+    ens[me] = pweight[0, 0] * total[1:]
 
     @pl.loop(1, pairs)
     def _(o):
@@ -739,20 +784,20 @@
         def _():
             (g0_lo, g0_hi)[side].wait_send()
             (g1_lo, g1_hi)[side].wait_send()
+            (e1_lo, e1_hi)[side].wait_send()
 
     index_copy.wait_send()
     on_chip(sent)
     for far in range(4):
         crossing(far, sent, True)
     crossing(0, sent, False)
-    crossing(3, sent, False)
-
-    for i in range(4):
+
+    for i in range(2):
         @pl.when(h1_sends[i])
         def _():
             h1_copy(i).wait_send()
 
-    for i, step in enumerate((-3, -2, -1, 1, 2, 3)):
+    for i, step in enumerate((-2, -1, 1, 2)):
         @pl.when(inside(step))
         def _():
             h2_copy(i).wait_send()
@@ -794,9 +839,10 @@
             scratch_shapes=[
                 *[vmem((8, 256, 256), BF16)] * 8,
                 vmem((256, 256), BF16),
+                vmem((15, 128, 128), BF16),
                 vmem((2, 2, 256, 128), F32),
                 pltpu.SMEM((1, 2), jnp.int32),
-                pltpu.SMEM((1,), F32),
+                pltpu.SMEM((1, 1), F32),
                 pltpu.SMEM((1, 2), jnp.int32),
                 vmem((4, 4, 128, 128), F32),
                 field, field, field,
@@ -805,6 +851,7 @@
                 vmem((6, 128, 128), F32),
                 vmem((2, 64, 128), F32), vmem((2, 64, 128), F32),
                 vmem((6, 128, 128), F32),
+                vmem((4, 128, 128), F32), vmem((2, 2, 128, 128), F32),
                 level2, level2, level2,
                 vmem((5, 64, 128), F32),
                 vmem((5, 64, 128), F32),
@@ -818,9 +865,10 @@
                 dma((1,)), dma((1,)),
                 dma((2, 4)), dma((2, 4)),
                 dma((2,)), dma((2,)),
+                dma((2,)), dma((2,)),
+                dma((2,)), dma((2,)),
+                dma((2,)), dma((2,)),
                 dma((4,)), dma((4,)),
-                dma((2,)), dma((2,)),
-                dma((6,)), dma((6,)),
                 dma((gz,)), dma((gz,)),
                 dma((gz,)), dma((gz,)),
                 dma((pairs,)), dma((pairs,)),
@@ -829,7 +877,7 @@
                 collective_id=0, has_side_effects=True, vmem_limit_bytes=48 * 1024 * 1024
             ),
             name="vcycle",
-        )(pair_index, pair_weight, orbitals)
+        )(pltpu.with_memory_space_constraint(pair_index, pltpu.HBM), pair_weight.reshape(1, 1), orbitals)
         return potential, norm.reshape(1), energy.reshape(1)
 
     return jax.shard_map(

time: 65 us -> 56.5 us (0.87)
  Pallas kernels: 58.1 us -> 50.3 us
    pallas_call x1, Pallas kernels: 58.1 us -> 50.3 us  [per_device(): pl.pallas_call(functools.partial(kernel, gz, pairs), out_shape=(jax.Shape...]
    unnamed x3 -> x1, local copies, waits for them, and re-layouts: 1.97 us -> 1.32 us
where the time goes in v4:
time: 56.5 us; the launch traced here: 56.3 us
  Pallas kernels  50.3 us (89%)
  between operations  4.74 us (8%)
  local copies, waits for them, and re-layouts  1.32 us (2%)
    pallas_call x1, Pallas kernels, per_device(): pl.pallas_call(functools.partial(kernel, gz, pairs), out_shape=(jax.Shape...  50.3 us
    unnamed x1, local copies, waits for them, and re-layouts  1.32 us

profile of v4, /device:TPU:1, one launch (start us, length us, event | category | flops | bytes accessed | tf_op | source)
XLA Modules:
  0.0 56.3 jit_solution(7592735367319865507)
XLA Ops:
  1.3 50.3 %vcycle.1 = (f32[1,8,256,256]{3,2,1,0:T(8,128)S(1)}, f32[1,1]{1,0:T(1,128)}, f32[1,1]{1,0:T(1,128)}) custom-call(s32[1,2]{1,0:T(1,128)} %index_in.1, f32[1,1]{1,0:T(1,128)} %bitcast.3.weight_in, bf16[8,8,256,256]{3,2,1,0:T(8,128)(2,1)} %orbitals.1), custom_call_target="tpu_custom_call" | custom-call | tf_op jit(solution)/shard_map/vcycle/pallas_call | solution.py:822
  51.5 1.3 %copy.10 = f32[1,8,256,256]{3,2,1,0:T(8,128)} copy(f32[1,8,256,256]{3,2,1,0:T(8,128)S(1)} %get-tuple-element.12) | data formatting | bytes 4194304

commit v5 on v4

--- a/solution.py
+++ b/solution.py
@@ -10,7 +10,7 @@
 MESH = pl.DeviceIdType.MESH
 F32, BF16 = jnp.float32, jnp.bfloat16
 PAD = 8
-EARLY = 0
+EARLY = 1
 CH = 32
 NINTH = 1.0 / 9.0
 N81 = 1.0 / 81.0
@@ -92,8 +92,8 @@
     gz, pairs,
     index_in, weight_in, orbitals, pot, res_out, en_out,
     orb0, orb1, orb2, orb3, orb4, orb5, orb6, orb7, px, mats, tmp, pidx, pweight, pidx2, fx, f, a, b, g0, g0o, s1, a1, b1, t1, g1, g1o, pe1, e1, e1h,
-    s2, a2, b2, t2, pe2, t3, s3, a3, b3, sums, ens,
-    scalar_sem, orb_sem, ixs, ixr, fs, fr, g0s, g0r, h1s, h1r, g1s, g1r, e1s, e1r, h2s, h2r, t3s, t3r, ss, sr, es, er,
+    s2, a2, b2, t2, pe2, t3, s3, a3, b3, prods, sums, ens,
+    scalar_sem, orb_sem, ixs, ixr, fs, fr, g0s, g0r, h1s, h1r, g1s, g1r, e1s, e1r, h2s, h2r, t3s, t3r, ps, pr, ss, sr, es, er,
 ):
     d = lax.axis_index("gz")
     me = lax.axis_index("pair")
@@ -679,10 +679,41 @@
     def above(last):
         return jnp.where(has_hi, last, 7)
 
-    f_wait(0)
+    f_wait(0, 1)
     w_plane(4, True, True)
     w_plane(11, True, True)
 
+    @pl.when(has_hi)
+    def _():
+        w_plane(12, True, True)
+
+    def products(z, carry):
+        plain, edges = carry
+        for r in range(0, 128, CH):
+            c, src, up = center(a, z, r, CH), center(f, z, r, CH), center(a, z + 1, r, CH)
+            for ph in range(4):
+                plain = plain + fold(c[ph] * (src[ph] - (3.0 * N81) * c[ph]))
+            e = c[0] * c[1] + c[2] * c[3] + (c[0] * c[2] + c[1] * c[3])
+            e = e + (c[1] * from_right(c[0]) + c[3] * from_right(c[2]))
+            e = e + (c[2] * rows(a, z, 0, r, CH, 1) + c[3] * rows(a, z, 1, r, CH, 1))
+            for ph in range(4):
+                e = e + c[ph] * up[ph]
+            edges = edges + fold(e)
+        return plain, edges
+
+    zero = jnp.zeros((8, 128), F32)
+    plain, edges = lax.fori_loop(4, 12, products, (zero, zero))
+    coarse = zero
+    for j in range(4):
+        coarse = coarse + fold(s1[5 + j, pl.ds(PAD, 128), :] * e1[j])
+    part = (2.0 * N81) * (plain + N81 * edges) + 2.0 * coarse
+    prods[d] = part.sum(axis=0, keepdims=True)
+
+    @pl.loop(1, gz)
+    def _(o):
+        remote(prods.at[d], prods.at[d], ps.at[o], pr.at[d], gz=lax.rem(d + o, gz)).start()
+
+
     @pl.loop(0, 8)
     def _(z):
         correct(z + 4, e1, z // 2)
@@ -690,7 +721,7 @@
     sweep0(a, b, 1, 6)
     sweep0(b, a, 2, 5)
 
-    f_wait(1, 2, 3)
+    f_wait(2, 3)
 
     @pl.loop(below(-3) + 4, 4)
     def _(z):
@@ -717,26 +748,35 @@
     sweep0(b, a, below(-1), 1)
     sweep0(b, a, 6, above(8))
 
-    def final(z, carry):
-        squares, products = carry
+    def final(z, squares):
         for r in range(0, 128, CH):
             c = center(a, z, r, CH)
             nb = nbxy0(a, z, r, CH, c)
             for ph in range(4):
                 t = nb[ph] + (rows(a, z - 1, ph, r, CH) + rows(a, z + 1, ph, r, CH))
-                src = rows(f, z, ph, r, CH)
-                left = (src - 6.0 * c[ph]) + t
+                left = (rows(f, z, ph, r, CH) - 6.0 * c[ph]) + t
                 squares = squares + fold(left * left)
-                products = products + fold(src * c[ph])
-        return squares, products
-
-    zero = jnp.zeros((8, 128), F32)
-    squares, products = lax.fori_loop(4, 12, final, (zero, zero))
-    sums[d] = jnp.concatenate([squares.sum(axis=0, keepdims=True), products.sum(axis=0, keepdims=True)], axis=0)
+        return squares
+
+    sums[d] = lax.fori_loop(4, 12, final, zero).sum(axis=0, keepdims=True)
 
     @pl.loop(1, gz)
     def _(o):
         remote(sums.at[d], sums.at[d], ss.at[o], sr.at[d], gz=lax.rem(d + o, gz)).start()
+
+    @pl.loop(1, gz)
+    def _(o):
+        peer = lax.rem(d + o, gz)
+        remote(prods.at[peer], prods.at[peer], ps.at[o], pr.at[peer], gz=peer).wait_recv()
+
+    total = prods[0]
+    for e in range(1, gz):
+        total = total + prods[e]
+    ens[me] = pweight[0, 0] * total
+
+    @pl.loop(1, pairs)
+    def _(o):
+        remote(ens.at[me], ens.at[me], es.at[o], er.at[me], pair=lax.rem(me + o, pairs)).start()
 
     px[...] = selection((256, 256), lambda i, j: i == (j & 1) * 128 + (j >> 1))
 
@@ -761,13 +801,7 @@
     for e in range(1, gz):
         total = total + sums[e]
     cells = 1.0 / (gz * 8 * 256 * 256)
-    ens[me] = pweight[0, 0] * total[1:]
-
-    @pl.loop(1, pairs)
-    def _(o):
-        remote(ens.at[me], ens.at[me], es.at[o], er.at[me], pair=lax.rem(me + o, pairs)).start()
-
-    res_out[...] = jnp.sqrt(jnp.sum(total[:1], axis=1, keepdims=True) * cells)
+    res_out[...] = jnp.sqrt(jnp.sum(total, axis=1, keepdims=True) * cells)
 
     @pl.loop(1, pairs)
     def _(o):
@@ -806,6 +840,7 @@
     def _(o):
         t3_copy(o).wait_send()
         remote(sums.at[d], sums.at[d], ss.at[o], sr.at[d], gz=lax.rem(d + o, gz)).wait_send()
+        remote(prods.at[d], prods.at[d], ps.at[o], pr.at[d], gz=lax.rem(d + o, gz)).wait_send()
 
     @pl.loop(1, pairs)
     def _(o):
@@ -858,7 +893,7 @@
                 vmem((gz, 40, 128), F32),
                 vmem((4, 32, 128), F32),
                 level3, level3,
-                vmem((gz, 2, 128), F32),
+                vmem((gz, 1, 128), F32), vmem((gz, 1, 128), F32),
                 vmem((pairs, 1, 128), F32),
                 dma((2,)),
                 dma((8,)),
@@ -871,6 +906,7 @@
                 dma((4,)), dma((4,)),
                 dma((gz,)), dma((gz,)),
                 dma((gz,)), dma((gz,)),
+                dma((gz,)), dma((gz,)),
                 dma((pairs,)), dma((pairs,)),
             ],
             compiler_params=pltpu.CompilerParams(

time: 56.5 us -> 51.2 us (0.906)
  Pallas kernels: 50.3 us -> 45 us
    pallas_call x1, Pallas kernels: 50.3 us -> 45 us  [per_device(): pl.pallas_call(functools.partial(kernel, gz, pairs), out_shape=(jax.Shape...]
where the time goes in v5:
time: 51.2 us; the launch traced here: 51 us
  Pallas kernels  45 us (88%)
  between operations  4.74 us (9%)
  local copies, waits for them, and re-layouts  1.32 us (3%)
    pallas_call x1, Pallas kernels, per_device(): pl.pallas_call(functools.partial(kernel, gz, pairs), out_shape=(jax.Shape...  45 us
    unnamed x1, local copies, waits for them, and re-layouts  1.32 us

profile of v5, /device:TPU:1, one launch (start us, length us, event | category | flops | bytes accessed | tf_op | source)
XLA Modules:
  0.0 51.0 jit_solution(9667439182885457293)
XLA Ops:
  1.3 45.0 %vcycle.1 = (f32[1,8,256,256]{3,2,1,0:T(8,128)S(1)}, f32[1,1]{1,0:T(1,128)}, f32[1,1]{1,0:T(1,128)}) custom-call(s32[1,2]{1,0:T(1,128)} %index_in.1, f32[1,1]{1,0:T(1,128)} %bitcast.3.weight_in, bf16[8,8,256,256]{3,2,1,0:T(8,128)(2,1)} %orbitals.1), custom_call_target="tpu_custom_call" | custom-call | tf_op jit(solution)/shard_map/vcycle/pallas_call | solution.py:857
  46.3 1.3 %copy.10 = f32[1,8,256,256]{3,2,1,0:T(8,128)} copy(f32[1,8,256,256]{3,2,1,0:T(8,128)S(1)} %get-tuple-element.12) | data formatting | bytes 4194304

commit v6 on v5

--- a/solution.py
+++ b/solution.py
@@ -10,7 +10,7 @@
 MESH = pl.DeviceIdType.MESH
 F32, BF16 = jnp.float32, jnp.bfloat16
 PAD = 8
-EARLY = 1
+EARLY = True
 CH = 32
 NINTH = 1.0 / 9.0
 N81 = 1.0 / 81.0
@@ -91,9 +91,9 @@
 def kernel(
     gz, pairs,
     index_in, weight_in, orbitals, pot, res_out, en_out,
-    orb0, orb1, orb2, orb3, orb4, orb5, orb6, orb7, px, mats, tmp, pidx, pweight, pidx2, fx, f, a, b, g0, g0o, s1, a1, b1, t1, g1, g1o, pe1, e1, e1h,
+    orb0, orb1, orb2, orb3, orb4, orb5, orb6, orb7, px, mats, tmp, pidx, pweight, pidx2, fx, relay, f, a, b, g0, g0o, s1, a1, b1, t1, g1, g1o, pe1, e1, e1h,
     s2, a2, b2, t2, pe2, t3, s3, a3, b3, prods, sums, ens,
-    scalar_sem, orb_sem, ixs, ixr, fs, fr, g0s, g0r, h1s, h1r, g1s, g1r, e1s, e1r, h2s, h2r, t3s, t3r, ps, pr, ss, sr, es, er,
+    scalar_sem, orb_sem, ixs, ixr, ys, yr, yf, fs, fr, g0s, g0r, h1s, h1r, g1s, g1r, e1s, e1r, h2s, h2r, t3s, t3r, ps, pr, ss, sr, es, er,
 ):
     d = lax.axis_index("gz")
     me = lax.axis_index("pair")
@@ -114,7 +114,7 @@
     weight_load = pltpu.make_async_copy(weight_in, pweight, scalar_sem.at[1])
     index_load.start()
     weight_load.start()
-    for z in (0, 7, 1, 6, 2, 5, 3, 4):
+    for z in range(8):
         orb_copy(z).start()
     barrier = pltpu.get_barrier_semaphore()
 
@@ -134,6 +134,15 @@
     @pl.when(has_across)
     def _():
         pl.semaphore_signal(barrier, inc=1, device_id={"gz": across, "pair": other}, device_id_type=MESH)
+
+    turn = lax.rem(d, 4)
+    straight = jnp.logical_or(turn == 1, turn == 2)
+    diagonal = jnp.logical_not(straight)
+    partner = jnp.where(turn == 0, d + 3, d - 3)
+
+    @pl.when(diagonal)
+    def _():
+        pl.semaphore_signal(barrier, inc=1, device_id={"gz": partner, "pair": other}, device_id_type=MESH)
 
     px[...] = selection((256, 256), lambda i, j: j == (i & 1) * 128 + (i >> 1))
     pad0 = jnp.zeros((4, PAD, 128), F32)
@@ -220,14 +229,6 @@
 
     index_load.wait()
     weight_load.wait()
-    for i, z in enumerate((0, 7, 1, 6, 2, 5, 3, 4)):
-        orb_copy(z).wait()
-
-        def put(ph, value):
-            f[z + 4, ph, pl.ds(PAD, 128), :] = value
-
-        density(z, pidx, i % 2, put)
-
     def w_plane(z, lo, hi):
         for r in range(0, 128, CH):
             c = center(f, z, r, CH)
@@ -240,10 +241,19 @@
                     t = t + rows(f, z + 1, ph, r, CH)
                 a[z, ph, pl.ds(PAD + r, CH), :] = t
 
-    w_plane(4, False, True)
+    for i, z in enumerate(range(8)):
+        orb_copy(z).wait()
+
+        def put(ph, value):
+            f[z + 4, ph, pl.ds(PAD, 128), :] = value
+
+        density(z, pidx, i % 2, put)
+        if z:
+            w_plane(z + 3, z > 1, True)
+
     w_plane(11, True, False)
 
-    pl.semaphore_wait(barrier, gz - 1 + pairs - 1 + has_across.astype(jnp.int32))
+    pl.semaphore_wait(barrier, gz - 1 + pairs - 1 + has_across.astype(jnp.int32) + diagonal.astype(jnp.int32))
 
     index_copy = remote(pidx, pidx2, ixs.at[0], ixr.at[0], pair=other)
     index_copy.start()
@@ -270,10 +280,6 @@
     @pl.when(has_hi)
     def _():
         g0_hi.start()
-
-    turn = lax.rem(d, 4)
-    straight = jnp.logical_or(turn == 1, turn == 2)
-    diagonal = jnp.logical_not(straight)
 
     def f_copy(side, far, of_other):
         k = far if side == 0 else 3 - far
@@ -295,17 +301,33 @@
                     act(side, far, False)
 
     def crossing(far, act, of_other, only=True):
+        kind = {
+            (0, False): diagonal, (3, False): straight,
+            (0, True): straight, (1, True): True, (2, True): straight,
+        }.get((far, of_other))
+        if kind is None:
+            return
         for side, cond in ((0, jnp.logical_and(even, has_lo)), (1, jnp.logical_and(jnp.logical_not(even), has_hi))):
-            cond = jnp.logical_and(cond, only)
-            if far == 0:
-                cond = jnp.logical_and(cond, straight if of_other else diagonal)
-            elif not of_other:
-                continue
-
-            @pl.when(cond)
+            @pl.when(jnp.logical_and(cond, jnp.logical_and(kind, only)))
             def _():
                 act(side, far, of_other)
 
+    relays = ((0, jnp.logical_and(turn == 0, has_lo), jnp.logical_and(turn == 0, d < gz - 4), -4),
+              (1, jnp.logical_and(turn == 3, has_hi), jnp.logical_and(turn == 3, d >= 4), 4))
+
+    def to_relay(side, far, step):
+        k = far if side == 0 else 3 - far
+        return remote(
+            fx.at[k], relay.at[far - 2], ys.at[far - 2], yr.at[far - 2], gz=jnp.clip(d + step, 0, gz - 1), pair=me
+        )
+
+    def hand_on(side, far):
+        there = 12 + far if side == 0 else 3 - far
+        return remote(
+            relay.at[far - 2], f.at[there, :, pl.ds(PAD, 128), :], yf.at[far - 2], fr.at[1 - side, far],
+            gz=jnp.clip(partner, 0, gz - 1), pair=other,
+        )
+
     def begin(side, far, of_other):
         f_copy(side, far, of_other).start()
 
@@ -314,10 +336,6 @@
 
     crossing(0, begin, False)
     on_chip(begin)
-
-    @pl.loop(5, 11)
-    def _(z):
-        w_plane(z, True, True)
 
     for ph in range(4):
         a[3, ph, pl.ds(PAD, 128), :] = flo * f[4, ph, pl.ds(PAD, 128), :]
@@ -412,8 +430,8 @@
     for far in range(4):
         for side, cond in ((0, even), (1, jnp.logical_not(even))):
             k = far if side == 0 else 3 - far
-            if far == 0:
-                cond = jnp.logical_and(cond, straight)
+            if far in (0, 3):
+                cond = jnp.logical_and(cond, straight if far == 0 else diagonal)
 
             def put_other(ph, value):
                 fx[k, ph] = value
@@ -422,7 +440,12 @@
             def _():
                 density(k + 4 * side, pidx2, far % 2, put_other)
 
-        crossing(far, begin, True, straight if far > EARLY else True)
+        crossing(far, begin, True, True if EARLY else straight)
+        if far >= 2:
+            for side, cond, _, step in relays:
+                @pl.when(cond)
+                def _():
+                    to_relay(side, far, step).start()
 
     @pl.when(has_lo)
     def _():
@@ -518,14 +541,22 @@
         def _():
             h2_copy(i).start()
 
+    crossing(3, begin, False)
+
 
     @pl.loop(1, gz)
     def _(o):
         peer = lax.rem(d + o, gz)
         remote(t3.at[peer], t3.at[peer], t3s.at[o], t3r.at[peer], gz=peer).wait_recv()
 
-    for far in range(EARLY + 1, 4):
-        crossing(far, begin, True, diagonal)
+    if not EARLY:
+        crossing(1, begin, True, diagonal)
+    for far in (2, 3):
+        for side, _, cond, step in relays:
+            @pl.when(cond)
+            def _():
+                to_relay(side, far, step).wait_recv()
+                hand_on(side, far).start()
 
     lane32 = lane_iota((32, 128))
     for q in range(4):
@@ -825,6 +856,16 @@
     for far in range(4):
         crossing(far, sent, True)
     crossing(0, sent, False)
+    crossing(3, sent, False)
+    for far in (2, 3):
+        for side, first, second, step in relays:
+            @pl.when(first)
+            def _():
+                to_relay(side, far, step).wait_send()
+
+            @pl.when(second)
+            def _():
+                hand_on(side, far).wait_send()
 
     for i in range(2):
         @pl.when(h1_sends[i])
@@ -880,6 +921,7 @@
                 pltpu.SMEM((1, 1), F32),
                 pltpu.SMEM((1, 2), jnp.int32),
                 vmem((4, 4, 128, 128), F32),
+                vmem((2, 4, 128, 128), F32),
                 field, field, field,
                 vmem((2, 128, 128), F32), vmem((2, 128, 128), F32),
                 level1, level1, level1,
@@ -898,6 +940,7 @@
                 dma((2,)),
                 dma((8,)),
                 dma((1,)), dma((1,)),
+                dma((2,)), dma((2,)), dma((2,)),
                 dma((2, 4)), dma((2, 4)),
                 dma((2,)), dma((2,)),
                 dma((2,)), dma((2,)),

time: 51.2 us -> 49.9 us (0.975)
  Pallas kernels: 45 us -> 43.7 us
    pallas_call x1, Pallas kernels: 45 us -> 43.7 us  [per_device(): pl.pallas_call(functools.partial(kernel, gz, pairs), out_shape=(jax.Shape...]
where the time goes in v6:
time: 49.9 us; the launch traced here: 49.8 us
  Pallas kernels  43.7 us (88%)
  between operations  4.74 us (9%)
  local copies, waits for them, and re-layouts  1.32 us (3%)
    pallas_call x1, Pallas kernels, per_device(): pl.pallas_call(functools.partial(kernel, gz, pairs), out_shape=(jax.Shape...  43.7 us
    unnamed x1, local copies, waits for them, and re-layouts  1.32 us

profile of v6, /device:TPU:1, one launch (start us, length us, event | category | flops | bytes accessed | tf_op | source)
XLA Modules:
  0.0 49.8 jit_solution(13025585966871532600)
XLA Ops:
  1.3 43.7 %vcycle.1 = (f32[1,8,256,256]{3,2,1,0:T(8,128)S(1)}, f32[1,1]{1,0:T(1,128)}, f32[1,1]{1,0:T(1,128)}) custom-call(s32[1,2]{1,0:T(1,128)} %index_in.1, f32[1,1]{1,0:T(1,128)} %bitcast.3.weight_in, bf16[8,8,256,256]{3,2,1,0:T(8,128)(2,1)} %orbitals.1), custom_call_target="tpu_custom_call" | custom-call | tf_op jit(solution)/shard_map/vcycle/pallas_call | solution.py:898
  45.0 1.3 %copy.10 = f32[1,8,256,256]{3,2,1,0:T(8,128)} copy(f32[1,8,256,256]{3,2,1,0:T(8,128)S(1)} %get-tuple-element.12) | data formatting | bytes 4194304

commit v7 on v6

--- a/solution.py
+++ b/solution.py
@@ -92,8 +92,8 @@
     gz, pairs,
     index_in, weight_in, orbitals, pot, res_out, en_out,
     orb0, orb1, orb2, orb3, orb4, orb5, orb6, orb7, px, mats, tmp, pidx, pweight, pidx2, fx, relay, f, a, b, g0, g0o, s1, a1, b1, t1, g1, g1o, pe1, e1, e1h,
-    s2, a2, b2, t2, pe2, t3, s3, a3, b3, prods, sums, ens,
-    scalar_sem, orb_sem, ixs, ixr, ys, yr, yf, fs, fr, g0s, g0r, h1s, h1r, g1s, g1r, e1s, e1r, h2s, h2r, t3s, t3r, ps, pr, ss, sr, es, er,
+    s2, a2, b2, t2, pe2, t3, s3, a3, b3, kept, prods, sums, ens,
+    scalar_sem, orb_sem, ixs, ixr, ys, yr, yf, fs, fr, g0s, g0r, h1s, h1r, g1s, g1r, e1s, e1r, h2s, h2r, t3s, t3p, t3r, ps, pr, ss, sr, es, er,
 ):
     d = lax.axis_index("gz")
     me = lax.axis_index("pair")
@@ -418,13 +418,20 @@
         row = jnp.where(block8 == k, part[8 * k:8 * k + 8], row)
     t3[d, pl.ds(32, 8), :] = 0.5 * row
 
+    beside = jnp.where(even, d + 1, d - 1)
+
     def t3_copy(o):
-        to = lax.rem(d + o, gz)
-        return remote(t3.at[d], t3.at[d], t3s.at[o], t3r.at[d], gz=to)
-
-    @pl.loop(1, gz)
+        return remote(t3.at[d], t3.at[d], t3s.at[o], t3r.at[d], gz=lax.rem(d + 2 * o, gz))
+
+    def t3_pass(o):
+        e = lax.rem(d + 2 * o, gz)
+        return remote(t3.at[e], t3.at[e], t3p.at[o], t3r.at[e], gz=beside)
+
+    @pl.loop(1, gz // 2)
     def _(o):
         t3_copy(o).start()
+
+    t3_pass(0).start()
 
     index_copy.wait_recv()
     for far in range(4):
@@ -519,6 +526,12 @@
 
     h1_start()
 
+    @pl.loop(1, gz // 2)
+    def _(o):
+        e = lax.rem(d + 2 * o, gz)
+        remote(t3.at[e], t3.at[e], t3s.at[o], t3r.at[e], gz=e).wait_recv()
+        t3_pass(o).start()
+
     @pl.when(has_lo)
     def _():
         g1_hi.wait_recv()
@@ -544,10 +557,10 @@
     crossing(3, begin, False)
 
 
-    @pl.loop(1, gz)
-    def _(o):
-        peer = lax.rem(d + o, gz)
-        remote(t3.at[peer], t3.at[peer], t3s.at[o], t3r.at[peer], gz=peer).wait_recv()
+    @pl.loop(0, gz // 2)
+    def _(o):
+        e = lax.rem(beside + 2 * o, gz)
+        remote(t3.at[e], t3.at[e], t3p.at[o], t3r.at[e], gz=beside).wait_recv()
 
     if not EARLY:
         crossing(1, begin, True, diagonal)
@@ -596,87 +609,6 @@
 
     sweep3(a3, b3)
 
-    for i, step in enumerate((-2, -1, 1, 2)):
-        @pl.when(inside(-step))
-        def _():
-            h2_copy(i).wait_recv()
-
-    for p in range(1, 6):
-        at = d + p - 3
-        q = jnp.clip(at // 4, 0, 3)
-        e = split_dot(b3[q, pl.ds(PAD, 32), :], mats[8 + p])
-        pe2[p - 1, pl.ds(0, 32, stride=2), :] = e
-        pe2[p - 1, pl.ds(1, 32, stride=2), :] = e
-    for p in range(1, 6):
-        c = crow(s2, p, 0, 64)
-        w = 12.0 * c + nb2(s2, p, c)
-        a2[p, pl.ds(PAD, 64), :] = flag2[p] * (N81 * w + pe2[p - 1])
-
-    def sweep2(src, dst, p):
-        c = crow(src, p, 0, 64)
-        dst[p, pl.ds(PAD, 64), :] = flag2[p] * (
-            (1.0 / 3.0) * c + NINTH * (nb2(src, p, c) + crow(s2, p, 0, 64))
-        )
-
-    for p in range(2, 5):
-        sweep2(a2, b2, p)
-    for p in range(2, 5):
-        sweep2(b2, a2, p)
-
-    for i in range(2):
-        @pl.when(h1_recvs[i])
-        def _():
-            h1_copy(i).wait_recv()
-
-    for j in range(1, 5):
-        e = split_dot(a2[2 + j // 2, pl.ds(PAD, 64), :], mats[2 + j % 2])
-        pe1[j, pl.ds(0, 64, stride=2), :] = e
-        pe1[j, pl.ds(1, 64, stride=2), :] = e
-
-    def in_grid(z):
-        return jnp.where(z < 5, flo, jnp.where(z > 8, fhi, 1.0))
-
-    def nb1(ref, z, r, c):
-        return nbxy(ref, z, r, 64, c, 128) + (crow(ref, z - 1, r, 64) + crow(ref, z + 1, r, 64))
-
-    @pl.loop(3, 11, unroll=4)
-    def _(z):
-        flag = in_grid(z)
-        for r in range(0, 128, 64):
-            c = crow(s1, z, r, 64)
-            w = 12.0 * c + nb1(s1, z, r, c)
-            a1[z, pl.ds(PAD + r, 64), :] = flag * (N81 * w + pe1[(z - 1) // 2, pl.ds(r, 64), :])
-
-    @pl.loop(4, 10, unroll=3)
-    def _(z):
-        flag = in_grid(z)
-        for r in range(0, 128, 64):
-            c = crow(a1, z, r, 64)
-            t = nb1(a1, z, r, c) + crow(s1, z, r, 64)
-            b1[z, pl.ds(PAD + r, 64), :] = flag * ((1.0 / 3.0) * c + NINTH * t)
-
-    @pl.loop(5, 9, unroll=4)
-    def _(z):
-        for r in range(0, 128, 64):
-            c = crow(b1, z, r, 64)
-            t = nb1(b1, z, r, c) + crow(s1, z, r, 64)
-            e1[z - 5, pl.ds(r, 64), :] = (1.0 / 3.0) * c + NINTH * t
-
-    e1_lo = remote(
-        e1.at[pl.ds(0, 2)], e1h.at[1], e1s.at[0], e1r.at[1], gz=jnp.maximum(d - 1, 0)
-    )
-    e1_hi = remote(
-        e1.at[pl.ds(2, 2)], e1h.at[0], e1s.at[1], e1r.at[0], gz=jnp.minimum(d + 1, gz - 1)
-    )
-
-    @pl.when(has_lo)
-    def _():
-        e1_lo.start()
-
-    @pl.when(has_hi)
-    def _():
-        e1_hi.start()
-
     def f_wait(*which):
         @pl.when(has_lo)
         def _():
@@ -687,28 +619,6 @@
         def _():
             for far in which:
                 f_copy(0, far, False).wait_recv()
-
-    def correct(z, ref, k):
-        e = ref[k]
-        for ph in range(4):
-            a[z, ph, pl.ds(PAD, 128), :] = N81 * a[z, ph, pl.ds(PAD, 128), :] + e
-
-    def sweep0(src, dst, first, last):
-        @pl.loop(first + 4, last + 5)
-        def _(z):
-            for r in range(0, 128, CH):
-                c = center(src, z, r, CH)
-                nb = nbxy0(src, z, r, CH, c)
-                for ph in range(4):
-                    t = nb[ph] + (rows(src, z - 1, ph, r, CH) + rows(src, z + 1, ph, r, CH))
-                    t = t + rows(f, z, ph, r, CH)
-                    dst[z, ph, pl.ds(PAD + r, CH), :] = (1.0 / 3.0) * c[ph] + NINTH * t
-
-    def below(first):
-        return jnp.where(has_lo, first, 0)
-
-    def above(last):
-        return jnp.where(has_hi, last, 7)
 
     f_wait(0, 1)
     w_plane(4, True, True)
@@ -734,6 +644,113 @@
 
     zero = jnp.zeros((8, 128), F32)
     plain, edges = lax.fori_loop(4, 12, products, (zero, zero))
+    kept[0] = plain
+    kept[1] = edges
+
+    for i, step in enumerate((-2, -1, 1, 2)):
+        @pl.when(inside(-step))
+        def _():
+            h2_copy(i).wait_recv()
+
+    for p in range(1, 6):
+        at = d + p - 3
+        q = jnp.clip(at // 4, 0, 3)
+        e = split_dot(b3[q, pl.ds(PAD, 32), :], mats[8 + p])
+        pe2[p - 1, pl.ds(0, 32, stride=2), :] = e
+        pe2[p - 1, pl.ds(1, 32, stride=2), :] = e
+    for p in range(1, 6):
+        c = crow(s2, p, 0, 64)
+        w = 12.0 * c + nb2(s2, p, c)
+        a2[p, pl.ds(PAD, 64), :] = flag2[p] * (N81 * w + pe2[p - 1])
+
+    def sweep2(src, dst, p):
+        c = crow(src, p, 0, 64)
+        dst[p, pl.ds(PAD, 64), :] = flag2[p] * (
+            (1.0 / 3.0) * c + NINTH * (nb2(src, p, c) + crow(s2, p, 0, 64))
+        )
+
+    for p in range(2, 5):
+        sweep2(a2, b2, p)
+    for p in range(2, 5):
+        sweep2(b2, a2, p)
+
+    for i in range(2):
+        @pl.when(h1_recvs[i])
+        def _():
+            h1_copy(i).wait_recv()
+
+    for j in range(1, 5):
+        e = split_dot(a2[2 + j // 2, pl.ds(PAD, 64), :], mats[2 + j % 2])
+        pe1[j, pl.ds(0, 64, stride=2), :] = e
+        pe1[j, pl.ds(1, 64, stride=2), :] = e
+
+    def in_grid(z):
+        return jnp.where(z < 5, flo, jnp.where(z > 8, fhi, 1.0))
+
+    def nb1(ref, z, r, c):
+        return nbxy(ref, z, r, 64, c, 128) + (crow(ref, z - 1, r, 64) + crow(ref, z + 1, r, 64))
+
+    @pl.loop(3, 11, unroll=4)
+    def _(z):
+        flag = in_grid(z)
+        for r in range(0, 128, 64):
+            c = crow(s1, z, r, 64)
+            w = 12.0 * c + nb1(s1, z, r, c)
+            a1[z, pl.ds(PAD + r, 64), :] = flag * (N81 * w + pe1[(z - 1) // 2, pl.ds(r, 64), :])
+
+    @pl.loop(4, 10, unroll=3)
+    def _(z):
+        flag = in_grid(z)
+        for r in range(0, 128, 64):
+            c = crow(a1, z, r, 64)
+            t = nb1(a1, z, r, c) + crow(s1, z, r, 64)
+            b1[z, pl.ds(PAD + r, 64), :] = flag * ((1.0 / 3.0) * c + NINTH * t)
+
+    @pl.loop(5, 9, unroll=4)
+    def _(z):
+        for r in range(0, 128, 64):
+            c = crow(b1, z, r, 64)
+            t = nb1(b1, z, r, c) + crow(s1, z, r, 64)
+            e1[z - 5, pl.ds(r, 64), :] = (1.0 / 3.0) * c + NINTH * t
+
+    e1_lo = remote(
+        e1.at[pl.ds(0, 2)], e1h.at[1], e1s.at[0], e1r.at[1], gz=jnp.maximum(d - 1, 0)
+    )
+    e1_hi = remote(
+        e1.at[pl.ds(2, 2)], e1h.at[0], e1s.at[1], e1r.at[0], gz=jnp.minimum(d + 1, gz - 1)
+    )
+
+    @pl.when(has_lo)
+    def _():
+        e1_lo.start()
+
+    @pl.when(has_hi)
+    def _():
+        e1_hi.start()
+
+    def correct(z, ref, k):
+        e = ref[k]
+        for ph in range(4):
+            a[z, ph, pl.ds(PAD, 128), :] = N81 * a[z, ph, pl.ds(PAD, 128), :] + e
+
+    def sweep0(src, dst, first, last):
+        @pl.loop(first + 4, last + 5)
+        def _(z):
+            for r in range(0, 128, CH):
+                c = center(src, z, r, CH)
+                nb = nbxy0(src, z, r, CH, c)
+                for ph in range(4):
+                    t = nb[ph] + (rows(src, z - 1, ph, r, CH) + rows(src, z + 1, ph, r, CH))
+                    t = t + rows(f, z, ph, r, CH)
+                    dst[z, ph, pl.ds(PAD + r, CH), :] = (1.0 / 3.0) * c[ph] + NINTH * t
+
+    def below(first):
+        return jnp.where(has_lo, first, 0)
+
+    def above(last):
+        return jnp.where(has_hi, last, 7)
+
+    plain, edges = kept[0], kept[1]
     coarse = zero
     for j in range(4):
         coarse = coarse + fold(s1[5 + j, pl.ds(PAD, 128), :] * e1[j])
@@ -879,9 +896,16 @@
 
     @pl.loop(1, gz)
     def _(o):
-        t3_copy(o).wait_send()
         remote(sums.at[d], sums.at[d], ss.at[o], sr.at[d], gz=lax.rem(d + o, gz)).wait_send()
         remote(prods.at[d], prods.at[d], ps.at[o], pr.at[d], gz=lax.rem(d + o, gz)).wait_send()
+
+    @pl.loop(1, gz // 2)
+    def _(o):
+        t3_copy(o).wait_send()
+
+    @pl.loop(0, gz // 2)
+    def _(o):
+        t3_pass(o).wait_send()
 
     @pl.loop(1, pairs)
     def _(o):
@@ -935,6 +959,7 @@
                 vmem((gz, 40, 128), F32),
                 vmem((4, 32, 128), F32),
                 level3, level3,
+                vmem((2, 8, 128), F32),
                 vmem((gz, 1, 128), F32), vmem((gz, 1, 128), F32),
                 vmem((pairs, 1, 128), F32),
                 dma((2,)),
@@ -947,7 +972,7 @@
                 dma((2,)), dma((2,)),
                 dma((2,)), dma((2,)),
                 dma((4,)), dma((4,)),
-                dma((gz,)), dma((gz,)),
+                dma((gz,)), dma((gz,)), dma((gz,)),
                 dma((gz,)), dma((gz,)),
                 dma((gz,)), dma((gz,)),
                 dma((pairs,)), dma((pairs,)),

time: 49.9 us -> 47.5 us (0.952)
  Pallas kernels: 43.7 us -> 41.2 us
    pallas_call x1, Pallas kernels: 43.7 us -> 41.2 us  [per_device(): pl.pallas_call(functools.partial(kernel, gz, pairs), out_shape=(jax.Shape...]
where the time goes in v7:
time: 47.5 us; the launch traced here: 47.3 us
  Pallas kernels  41.2 us (87%)
  between operations  4.74 us (10%)
  local copies, waits for them, and re-layouts  1.32 us (3%)
    pallas_call x1, Pallas kernels, per_device(): pl.pallas_call(functools.partial(kernel, gz, pairs), out_shape=(jax.Shape...  41.2 us
    unnamed x1, local copies, waits for them, and re-layouts  1.32 us

profile of v7, /device:TPU:1, one launch (start us, length us, event | category | flops | bytes accessed | tf_op | source)
XLA Modules:
  0.0 47.3 jit_solution(1597842293398879668)
XLA Ops:
  1.3 41.2 %vcycle.1 = (f32[1,8,256,256]{3,2,1,0:T(8,128)S(1)}, f32[1,1]{1,0:T(1,128)}, f32[1,1]{1,0:T(1,128)}) custom-call(s32[1,2]{1,0:T(1,128)} %index_in.1, f32[1,1]{1,0:T(1,128)} %bitcast.3.weight_in, bf16[8,8,256,256]{3,2,1,0:T(8,128)(2,1)} %orbitals.1), custom_call_target="tpu_custom_call" | custom-call | tf_op jit(solution)/shard_map/vcycle/pallas_call | solution.py:922
  42.5 1.3 %copy.10 = f32[1,8,256,256]{3,2,1,0:T(8,128)} copy(f32[1,8,256,256]{3,2,1,0:T(8,128)S(1)} %get-tuple-element.12) | data formatting | bytes 4194304

commit v8 on v7

--- a/solution.py
+++ b/solution.py
@@ -90,7 +90,7 @@
 
 def kernel(
     gz, pairs,
-    index_in, weight_in, orbitals, pot, res_out, en_out,
+    index_in, weight_in, orbitals, pot, stats,
     orb0, orb1, orb2, orb3, orb4, orb5, orb6, orb7, px, mats, tmp, pidx, pweight, pidx2, fx, relay, f, a, b, g0, g0o, s1, a1, b1, t1, g1, g1o, pe1, e1, e1h,
     s2, a2, b2, t2, pe2, t3, s3, a3, b3, kept, prods, sums, ens,
     scalar_sem, orb_sem, ixs, ixr, ys, yr, yf, fs, fr, g0s, g0r, h1s, h1r, g1s, g1r, e1s, e1r, h2s, h2r, t3s, t3p, t3r, ps, pr, ss, sr, es, er,
@@ -624,6 +624,10 @@
     w_plane(4, True, True)
     w_plane(11, True, True)
 
+    @pl.when(has_lo)
+    def _():
+        w_plane(3, True, True)
+
     @pl.when(has_hi)
     def _():
         w_plane(12, True, True)
@@ -769,33 +773,6 @@
     sweep0(a, b, 1, 6)
     sweep0(b, a, 2, 5)
 
-    f_wait(2, 3)
-
-    @pl.loop(below(-3) + 4, 4)
-    def _(z):
-        w_plane(z, True, True)
-
-    @pl.loop(12, above(10) + 5)
-    def _(z):
-        w_plane(z, True, True)
-
-    @pl.when(has_lo)
-    def _():
-        e1_hi.wait_recv()
-        for z in range(-3, 0):
-            correct(z + 4, e1h.at[0], (z + 4) // 2)
-
-    @pl.when(has_hi)
-    def _():
-        e1_lo.wait_recv()
-        for z in range(8, 11):
-            correct(z + 4, e1h.at[1], (z - 8) // 2)
-
-    sweep0(a, b, below(-2), 0)
-    sweep0(a, b, 7, above(9))
-    sweep0(b, a, below(-1), 1)
-    sweep0(b, a, 6, above(8))
-
     def final(z, squares):
         for r in range(0, 128, CH):
             c = center(a, z, r, CH)
@@ -806,7 +783,37 @@
                 squares = squares + fold(left * left)
         return squares
 
-    sums[d] = lax.fori_loop(4, 12, final, zero).sum(axis=0, keepdims=True)
+    kept[0] = lax.fori_loop(7, 9, final, zero)
+
+    f_wait(2, 3)
+
+    @pl.loop(jnp.where(has_lo, 1, 3), 3)
+    def _(z):
+        w_plane(z, True, True)
+
+    @pl.loop(13, jnp.where(has_hi, 15, 13))
+    def _(z):
+        w_plane(z, True, True)
+
+    @pl.when(has_lo)
+    def _():
+        e1_hi.wait_recv()
+        for z in range(-3, 0):
+            correct(z + 4, e1h.at[0], (z + 4) // 2)
+
+    @pl.when(has_hi)
+    def _():
+        e1_lo.wait_recv()
+        for z in range(8, 11):
+            correct(z + 4, e1h.at[1], (z - 8) // 2)
+
+    sweep0(a, b, below(-2), 0)
+    sweep0(a, b, 7, above(9))
+    sweep0(b, a, below(-1), 1)
+    sweep0(b, a, 6, above(8))
+
+    squares = lax.fori_loop(4, 7, final, kept[0])
+    sums[d] = lax.fori_loop(9, 12, final, squares).sum(axis=0, keepdims=True)
 
     @pl.loop(1, gz)
     def _(o):
@@ -849,7 +856,7 @@
     for e in range(1, gz):
         total = total + sums[e]
     cells = 1.0 / (gz * 8 * 256 * 256)
-    res_out[...] = jnp.sqrt(jnp.sum(total, axis=1, keepdims=True) * cells)
+    stats[0:1, :] = jnp.zeros((1, 128), F32) + jnp.sqrt(jnp.sum(total, axis=1, keepdims=True) * cells)
 
     @pl.loop(1, pairs)
     def _(o):
@@ -859,7 +866,7 @@
     energy = ens[0]
     for e in range(1, pairs):
         energy = energy + ens[e]
-    en_out[...] = jnp.sum(energy, axis=1, keepdims=True) * (-0.5 * cells)
+    stats[1:2, :] = jnp.zeros((1, 128), F32) + jnp.sum(energy, axis=1, keepdims=True) * (-0.5 * cells)
 
     for cond, side in ((has_lo, 0), (has_hi, 1)):
         @pl.when(cond)
@@ -919,12 +926,11 @@
     level1, level2, level3 = vmem((14, 144, 128), F32), vmem((7, 80, 128), F32), vmem((4, 48, 128), F32)
 
     def per_device(orbitals, pair_index, pair_weight):
-        potential, norm, energy = pl.pallas_call(
+        potential, stats = pl.pallas_call(
             functools.partial(kernel, gz, pairs),
             out_shape=(
                 jax.ShapeDtypeStruct((1, 8, 256, 256), F32),
-                jax.ShapeDtypeStruct((1, 1), F32),
-                jax.ShapeDtypeStruct((1, 1), F32),
+                jax.ShapeDtypeStruct((2, 128), F32),
             ),
             in_specs=[
                 pl.BlockSpec(memory_space=pltpu.HBM),
@@ -932,7 +938,6 @@
                 pl.BlockSpec(memory_space=pl.ANY),
             ],
             out_specs=(
-                pl.BlockSpec(memory_space=pltpu.VMEM),
                 pl.BlockSpec(memory_space=pltpu.VMEM),
                 pl.BlockSpec(memory_space=pltpu.VMEM),
             ),
@@ -982,7 +987,7 @@
             ),
             name="vcycle",
         )(pltpu.with_memory_space_constraint(pair_index, pltpu.HBM), pair_weight.reshape(1, 1), orbitals)
-        return potential, norm.reshape(1), energy.reshape(1)
+        return potential, stats[0, :1], stats[1, :1]
 
     return jax.shard_map(
         per_device,

time: 47.5 us -> 43.7 us (0.920)
  between operations: 4.74 us -> 1.29 us
  Pallas kernels: 41.2 us -> 40.5 us
  local copies, waits for them, and re-layouts: 1.32 us -> 1.84 us
    pallas_call x1, Pallas kernels: 41.2 us -> 40.5 us  [per_device(): pl.pallas_call(functools.partial(kernel, gz, pairs), out_shape=(jax.Shape...]
    slice x0 -> x1, local copies, waits for them, and re-layouts: none -> 0.52 us  [per_device(): return (potential, stats[0, :1], stats[1, :1])]
where the time goes in v8:
time: 43.7 us; the launch traced here: 43.6 us
  Pallas kernels  40.5 us (93%)
  local copies, waits for them, and re-layouts  1.84 us (4%)
  between operations  1.29 us (3%)
    pallas_call x1, Pallas kernels, per_device(): pl.pallas_call(functools.partial(kernel, gz, pairs), out_shape=(jax.Shape...  40.5 us
    unnamed x1, local copies, waits for them, and re-layouts  1.32 us

profile of v8, /device:TPU:1, one launch (start us, length us, event | category | flops | bytes accessed | tf_op | source)
XLA Modules:
  0.0 43.6 jit_solution(16381685258194600493)
XLA Ops:
  1.3 40.5 %vcycle.1 = (f32[1,8,256,256]{3,2,1,0:T(8,128)S(1)}, f32[2,128]{1,0:T(2,128)S(1)}) custom-call(s32[1,2]{1,0:T(1,128)} %index_in.1, f32[1,1]{1,0:T(1,128)} %bitcast.3.weight_in, bf16[8,8,256,256]{3,2,1,0:T(8,128)(2,1)} %orbitals.1), custom_call_target="tpu_custom_call" | custom-call | tf_op jit(solution)/shard_map/vcycle/pallas_call | solution.py:929
  41.7 0.5 %fusion = (f32[1,1]{1,0:T(1,128)}, f32[1,1]{1,0:T(1,128)}) fusion(f32[2,128]{1,0:T(2,128)S(1)} %get-tuple-element.6), kind=kLoop, calls=%fused_computation | loop fusion | bytes 16 | tf_op jit(solution)/shard_map/slice | solution.py:990
  42.3 1.3 %copy.8 = f32[1,8,256,256]{3,2,1,0:T(8,128)} copy(f32[1,8,256,256]{3,2,1,0:T(8,128)S(1)} %get-tuple-element.12) | data formatting | bytes 4194304

commit v9 on v8

--- a/solution.py
+++ b/solution.py
@@ -376,7 +376,7 @@
     b1[4, pl.ds(PAD, 128), :] = flo * g0o[0]
     b1[9, pl.ds(PAD, 128), :] = fhi * g0o[1]
 
-    @pl.loop(3, 11, unroll=4)
+    @pl.loop(3, 11, unroll=8)
     def _(z):
         flag = jnp.where(z < 5, flo, jnp.where(z > 8, fhi, 1.0))
         for r in range(0, 128, 64):
@@ -384,7 +384,7 @@
             nb = nbxy(b1, z, r, 64, c, 128) + (crow(b1, z - 1, r, 64) + crow(b1, z + 1, r, 64))
             a1[z, pl.ds(PAD + r, 64), :] = flag * (12.0 * c + nb)
 
-    @pl.loop(0, 6, unroll=2)
+    @pl.loop(0, 6, unroll=3)
     def _(j):
         for r in range(0, 128, 64):
             out = None
@@ -694,7 +694,7 @@
     def nb1(ref, z, r, c):
         return nbxy(ref, z, r, 64, c, 128) + (crow(ref, z - 1, r, 64) + crow(ref, z + 1, r, 64))
 
-    @pl.loop(3, 11, unroll=4)
+    @pl.loop(3, 11, unroll=8)
     def _(z):
         flag = in_grid(z)
         for r in range(0, 128, 64):
@@ -702,7 +702,7 @@
             w = 12.0 * c + nb1(s1, z, r, c)
             a1[z, pl.ds(PAD + r, 64), :] = flag * (N81 * w + pe1[(z - 1) // 2, pl.ds(r, 64), :])
 
-    @pl.loop(4, 10, unroll=3)
+    @pl.loop(4, 10, unroll=6)
     def _(z):
         flag = in_grid(z)
         for r in range(0, 128, 64):
@@ -847,27 +847,6 @@
         for half in range(2):
             pot[0, z, :, pl.ds(128 * half, 128)] = tmp[z % 2, half]
 
-    @pl.loop(1, gz)
-    def _(o):
-        peer = lax.rem(d + o, gz)
-        remote(sums.at[peer], sums.at[peer], ss.at[o], sr.at[peer], gz=peer).wait_recv()
-
-    total = sums[0]
-    for e in range(1, gz):
-        total = total + sums[e]
-    cells = 1.0 / (gz * 8 * 256 * 256)
-    stats[0:1, :] = jnp.zeros((1, 128), F32) + jnp.sqrt(jnp.sum(total, axis=1, keepdims=True) * cells)
-
-    @pl.loop(1, pairs)
-    def _(o):
-        peer = lax.rem(me + o, pairs)
-        remote(ens.at[peer], ens.at[peer], es.at[o], er.at[peer], pair=peer).wait_recv()
-
-    energy = ens[0]
-    for e in range(1, pairs):
-        energy = energy + ens[e]
-    stats[1:2, :] = jnp.zeros((1, 128), F32) + jnp.sum(energy, axis=1, keepdims=True) * (-0.5 * cells)
-
     for cond, side in ((has_lo, 0), (has_hi, 1)):
         @pl.when(cond)
         def _():
@@ -901,18 +880,39 @@
         def _():
             h2_copy(i).wait_send()
 
+    @pl.loop(1, gz // 2)
+    def _(o):
+        t3_copy(o).wait_send()
+
+    @pl.loop(0, gz // 2)
+    def _(o):
+        t3_pass(o).wait_send()
+
+    @pl.loop(1, gz)
+    def _(o):
+        peer = lax.rem(d + o, gz)
+        remote(sums.at[peer], sums.at[peer], ss.at[o], sr.at[peer], gz=peer).wait_recv()
+
+    total = sums[0]
+    for e in range(1, gz):
+        total = total + sums[e]
+    cells = 1.0 / (gz * 8 * 256 * 256)
+    stats[0:1, :] = jnp.zeros((1, 128), F32) + jnp.sqrt(jnp.sum(total, axis=1, keepdims=True) * cells)
+
+    @pl.loop(1, pairs)
+    def _(o):
+        peer = lax.rem(me + o, pairs)
+        remote(ens.at[peer], ens.at[peer], es.at[o], er.at[peer], pair=peer).wait_recv()
+
+    energy = ens[0]
+    for e in range(1, pairs):
+        energy = energy + ens[e]
+    stats[1:2, :] = jnp.zeros((1, 128), F32) + jnp.sum(energy, axis=1, keepdims=True) * (-0.5 * cells)
+
     @pl.loop(1, gz)
     def _(o):
         remote(sums.at[d], sums.at[d], ss.at[o], sr.at[d], gz=lax.rem(d + o, gz)).wait_send()
         remote(prods.at[d], prods.at[d], ps.at[o], pr.at[d], gz=lax.rem(d + o, gz)).wait_send()
-
-    @pl.loop(1, gz // 2)
-    def _(o):
-        t3_copy(o).wait_send()
-
-    @pl.loop(0, gz // 2)
-    def _(o):
-        t3_pass(o).wait_send()
 
     @pl.loop(1, pairs)
     def _(o):

time: 43.7 us -> 42.9 us (0.982)
  Pallas kernels: 40.5 us -> 39.5 us
    pallas_call x1, Pallas kernels: 40.5 us -> 39.5 us  [per_device(): pl.pallas_call(functools.partial(kernel, gz, pairs), out_shape=(jax.Shape...]
where the time goes in v9:
time: 42.9 us; the launch traced here: 42.6 us
  Pallas kernels  39.5 us (92%)
  local copies, waits for them, and re-layouts  1.84 us (4%)
  between operations  1.29 us (3%)
    pallas_call x1, Pallas kernels, per_device(): pl.pallas_call(functools.partial(kernel, gz, pairs), out_shape=(jax.Shape...  39.5 us
    unnamed x1, local copies, waits for them, and re-layouts  1.32 us

profile of v9, /device:TPU:1, one launch (start us, length us, event | category | flops | bytes accessed | tf_op | source)
XLA Modules:
  0.0 42.6 jit_solution(14085634289468477458)
XLA Ops:
  1.3 39.5 %vcycle.1 = (f32[1,8,256,256]{3,2,1,0:T(8,128)S(1)}, f32[2,128]{1,0:T(2,128)S(1)}) custom-call(s32[1,2]{1,0:T(1,128)} %index_in.1, f32[1,1]{1,0:T(1,128)} %bitcast.3.weight_in, bf16[8,8,256,256]{3,2,1,0:T(8,128)(2,1)} %orbitals.1), custom_call_target="tpu_custom_call" | custom-call | tf_op jit(solution)/shard_map/vcycle/pallas_call | solution.py:929
  40.8 0.5 %fusion = (f32[1,1]{1,0:T(1,128)}, f32[1,1]{1,0:T(1,128)}) fusion(f32[2,128]{1,0:T(2,128)S(1)} %get-tuple-element.6), kind=kLoop, calls=%fused_computation | loop fusion | bytes 16 | tf_op jit(solution)/shard_map/slice | solution.py:990
  41.3 1.3 %copy.8 = f32[1,8,256,256]{3,2,1,0:T(8,128)} copy(f32[1,8,256,256]{3,2,1,0:T(8,128)S(1)} %get-tuple-element.12) | data formatting | bytes 4194304
